TPU v7x, 32 devices: a whole 2x2x4 slice. The times are simulated.
32 devices in a mesh: batch: 8 (over z, core), vocab: 4 (over y, x).
Axes of the slice: x: 2, y: 2, z: 4, core: 2. Of those that a mesh axis runs over, the one named last changes fastest.
Arguments:
- window_ids: int32 [3, 16, 8], P(None, 'batch'), may hold values from 0 to 16383
- pool_ids: int32 [3, 16, 8], P(None, 'batch'), may hold values from 0 to 16383
- accepted: int32 [2, 16], P(None, 'batch'), may hold values from 1 to 8
- converged: int32 [2, 16], P(None, 'batch'), may hold values 0 or 1
- cache_lens: int32 [16], P('batch'), may hold values from 1 to 128
- table: bfloat16 [16384, 4608], P(('batch', 'vocab')), may hold values from -0.29882812 to 0.29882812
- attn_gain: float32 [4608], replicated, may hold values from 0.25 to 1.75
- post_gain: float32 [4608], replicated, may hold values from 0.25 to 1.75
- final_gain: float32 [4608], replicated, may hold values from 0.25 to 1.75
- w_query: bfloat16 [4608, 1024], P(None, 'vocab'), may hold values from -0.09375 to 0.09375
- w_key: bfloat16 [4608, 512], P(None, 'vocab'), may hold values from -0.09375 to 0.09375
- w_value: bfloat16 [4608, 512], P(None, 'vocab'), may hold values from -0.09375 to 0.09375
- w_out: bfloat16 [1024, 4608], P('vocab'), may hold values from -0.1875 to 0.1875
- cache_keys: bfloat16 [16, 4, 128, 128], P('batch', 'vocab'), may hold values from -6 to 6
- cache_values: bfloat16 [16, 4, 128, 128], P('batch', 'vocab'), may hold values from -6 to 6
Outputs:
- log_total: float32 [3, 16, 8], P(None, 'batch')
- best_logit: float32 [3, 16, 8], P(None, 'batch')
- pool_score: float32 [3, 16, 8], P(None, 'batch')
Inputs may be any that keep to these rules, and one draw needn't show every extreme that they name: `converged`: 1 marks a window at its fixed point, whose tokens are all accepted.
All inputs are finite; a program needn't handle non-finite values. No bound on the sum of `converged` on one device may be relied on, other than what follows from the above.
Results may differ from a plain program's by a relative error of at most 0.00036.
Values may be sent and summed in bfloat16 or wider, within the bound.
No kernel may reach another device: no remote copies, remote signals or barrier semaphores. Data moves between devices by JAX's collectives and lax.ppermute only.
A program may use at most 128 MiB of HBM per device.

v0:
```python
import math

import jax
import jax.numpy as jnp
from jax import lax
from jax.sharding import PartitionSpec as P

epsilon = 1e-06
query_scalar = 144.0
score_cap = 50.0
logit_cap = 30.0


def normalize(values_in, gain):
    return (
        values_in
        * lax.rsqrt(jnp.mean(values_in * values_in, axis=-1, keepdims=True) + epsilon)
        * gain
    )


def rotate(values_in, positions):
    half_size = values_in.shape[-1] // 2
    freqs = 10000.0 ** (-jnp.arange(half_size, dtype=jnp.float32) / half_size)
    angles = positions.astype(jnp.float32)[..., None] * freqs
    cosine = jnp.cos(angles)
    sine = jnp.sin(angles)
    first_half = values_in[..., :half_size]
    second_half = values_in[..., half_size:]
    return jnp.concatenate(
        [first_half * cosine - second_half * sine, second_half * cosine + first_half * sine],
        axis=-1,
    )


def attend(queries, key_rows, value_rows, visible):
    scores = jnp.einsum("bwhgd,bhld->bhgwl", queries, key_rows, preferred_element_type=jnp.float32)
    scores = score_cap * jnp.tanh(scores / score_cap)
    weights = jnp.where(visible[:, None, None], jnp.exp(scores), 0.0)
    weight_sum = jnp.sum(weights, axis=-1, keepdims=True)
    rounded = lax.optimization_barrier(weights.astype(jnp.bfloat16))
    summed = jnp.einsum(
        "bhgwl,bhld->bwhgd", rounded, value_rows, preferred_element_type=jnp.float32
    )
    return (summed / jnp.moveaxis(weight_sum, 3, 1)).astype(jnp.bfloat16)


def per_device(
    window_ids,
    pool_ids,
    accepted,
    converged,
    cache_lens,
    table,
    attn_gain,
    post_gain,
    final_gain,
    w_query,
    w_key,
    w_value,
    w_out,
    cache_keys,
    cache_values,
):
    iter_count, local_batch, width = window_ids.shape
    model_width = table.shape[1]
    vocab_rows = table.shape[0]
    head_size = cache_keys.shape[3]
    kv_local = cache_keys.shape[1]
    cache_slots = cache_keys.shape[2]
    local_rows = local_batch * width
    vocab_devices = lax.axis_size("vocab")
    batch_index = lax.axis_index("batch")
    vocab_index = lax.axis_index("vocab")
    all_windows, all_pools = (
        lax.all_gather(window_ids, "batch", axis=1, tiled=True),
        lax.all_gather(pool_ids, "batch", axis=1, tiled=True),
    )
    total_batch = all_windows.shape[1]
    first_id = (batch_index * vocab_devices + vocab_index) * vocab_rows
    ordered = jnp.transpose(all_windows, (1, 2, 0)) - first_id
    inside = (ordered >= 0) & (ordered < vocab_rows)
    looked_up = jnp.take(table, jnp.clip(ordered, 0, vocab_rows - 1), axis=0)
    lookup_terms = jnp.where(inside[..., None], looked_up.astype(jnp.float32), 0.0)
    column_rows = lax.psum_scatter(
        lookup_terms.astype(jnp.bfloat16), "batch", scatter_dimension=0, tiled=True
    )
    embedded_all = lax.psum(column_rows, "vocab").astype(jnp.float32)
    taken = jnp.where(converged == 1, width, accepted)
    offset = cache_lens
    slots = jnp.arange(width, dtype=jnp.int32)
    cache_visible = (
        jnp.arange(cache_slots, dtype=jnp.int32)[None, None, :] < cache_lens[:, None, None]
    )
    own_visible = slots[None, None, :] <= slots[None, :, None]
    key_list = [cache_keys]
    value_list = [cache_values]
    mask_list = [jnp.broadcast_to(cache_visible, (local_batch, width, cache_slots))]
    vocab_iota = jnp.arange(vocab_rows, dtype=jnp.int32)
    totals_out = []
    best_out = []
    score_out = []
    for step in range(iter_count):
        embedded = embedded_all[:, :, step] * math.sqrt(model_width)
        normed = (
            normalize(embedded, attn_gain).astype(jnp.bfloat16).reshape(local_rows, model_width)
        )
        positions = (offset[:, None] + slots[None, :])[:, :, None]
        queries = jnp.dot(normed, w_query, preferred_element_type=jnp.float32).reshape(
            local_batch, width, 2 * kv_local, head_size
        )
        queries = (
            (rotate(queries, positions) / math.sqrt(query_scalar))
            .astype(jnp.bfloat16)
            .reshape(local_batch, width, kv_local, 2, head_size)
        )
        keys_now = jnp.dot(normed, w_key, preferred_element_type=jnp.float32).reshape(
            local_batch, width, kv_local, head_size
        )
        keys_now = rotate(keys_now, positions).astype(jnp.bfloat16).transpose(0, 2, 1, 3)
        values_now = jnp.dot(normed, w_value, preferred_element_type=jnp.float32).reshape(
            local_batch, width, kv_local, head_size
        )
        values_now = values_now.astype(jnp.bfloat16).transpose(0, 2, 1, 3)
        all_keys = jnp.concatenate(key_list + [keys_now], axis=2)
        all_values = jnp.concatenate(value_list + [values_now], axis=2)
        visible = jnp.concatenate(
            mask_list + [jnp.broadcast_to(own_visible, (local_batch, width, width))], axis=2
        )
        attended = attend(queries, all_keys, all_values, visible).reshape(
            local_rows, 2 * kv_local * head_size
        )
        branch = jnp.dot(attended, w_out, preferred_element_type=jnp.float32)
        residual = embedded.reshape(local_rows, model_width)
        whole_branch = lax.psum(branch, "vocab")
        hidden = residual + normalize(whole_branch, post_gain)
        final_rows = normalize(hidden, final_gain).astype(jnp.bfloat16)
        pool_local = all_pools[step].reshape(total_batch * width) - first_id
        raw_logits = lax.dot_general(
            lax.all_gather(final_rows, "batch", axis=0, tiled=True),
            table,
            (((1,), (1,)), ((), ())),
            preferred_element_type=jnp.float32,
        )
        logits = logit_cap * jnp.tanh(raw_logits / logit_cap)
        exp_sums = jnp.sum(jnp.exp(logits), axis=-1)
        largest = jnp.max(logits, axis=-1)
        chosen = jnp.sum(
            jnp.where(vocab_iota[None, :] == pool_local[:, None], logits, 0.0), axis=-1
        )
        own_start = batch_index * local_rows
        sums_column, picks_column = (
            lax.psum_scatter(exp_sums, "batch", scatter_dimension=0, tiled=True),
            lax.psum_scatter(chosen, "batch", scatter_dimension=0, tiled=True),
        )
        sums_own, picks_own = lax.psum((sums_column, picks_column), "vocab")
        tops_joint = lax.pmax(largest, ("batch", "vocab"))
        tops_own = lax.dynamic_slice_in_dim(tops_joint, own_start, local_rows)
        log_sum = jnp.log(sums_own)
        totals_out.append(log_sum.reshape(local_batch, width))
        best_out.append(tops_own.reshape(local_batch, width))
        score_out.append((picks_own - log_sum).reshape(local_batch, width))
        if step + 1 < iter_count:
            key_list.append(keys_now)
            value_list.append(values_now)
            mask_list.append(
                jnp.broadcast_to(
                    slots[None, None, :] < taken[step][:, None, None], (local_batch, width, width)
                )
            )
            offset = offset + taken[step]
    return (jnp.stack(totals_out), jnp.stack(best_out), jnp.stack(score_out))


def solution(mesh):
    return jax.shard_map(
        per_device,
        mesh=mesh,
        in_specs=(
            P(None, "batch", None),
            P(None, "batch", None),
            P(None, "batch"),
            P(None, "batch"),
            P("batch"),
            P(("batch", "vocab"), None),
            P(),
            P(),
            P(),
            P(None, "vocab"),
            P(None, "vocab"),
            P(None, "vocab"),
            P("vocab", None),
            P("batch", "vocab", None, None),
            P("batch", "vocab", None, None),
        ),
        out_specs=(P(None, "batch", None), P(None, "batch", None), P(None, "batch", None)),
        check_vma=False,
    )
```

profile of v0, /device:TPU:10, one launch (start us, length us, event | category | flops | bytes accessed | tf_op | source)
XLA Modules:
  0.0 360.0 jit_solution(6029630634133774123)
XLA Ops:
  8.1 14.3 %all_gather.15 = s32[3,16,8]{2,0,1:T(4,128)S(1)} all-gather(s32[3,2,8]{2,0,1:T(4,128)S(1)} %copy.76), channel_id=1, replica_groups=mesh['batch'=8,'vocab'=4] {'batch'}, dimensions={1}, use_global_device_ids=true | all-gather | bytes 1728 | tf_op jit(solution)/shard_map/all_gather | solution.py:76
  22.8 12.2 %gather_fusion = bf16[384,4608]{1,0:T(8,128)(2,1)} fusion(bf16[512,4608]{1,0:T(8,128)(2,1)} %param.20, s32[1024]{0:T(1024)S(1)} %pad_clamp_fusion), kind=kCustom, calls=%fused_computation | custom fusion | bytes 7079424 | tf_op jit(solution)/shard_map/jit(_take)/gather | solution.py:83
  35.0 7.3 %reshape.718 = bf16[16,8,3,4608]{3,2,1,0:T(4,128)(2,1)} reshape(bf16[384,4608]{1,0:T(8,128)(2,1)} %gather_fusion) | data formatting | bytes 7077888 | tf_op jit(solution)/shard_map/jit(_take)/gather | solution.py:83
  42.4 6.3 %select_convert_fusion = bf16[16,8,3,4608]{3,1,2,0:T(8,128)(2,1)} fusion(bf16[16,8,3,4608]{3,2,1,0:T(4,128)(2,1)} %reshape.718, pred[16,8,3]{1,2,0:T(4,128)(4,1)S(1)} %copy.79, pred[16,8,3]{1,2,0:T(4,128)(4,1)S(1)} %copy.78), kind=kLoop, calls=%fused_computation.1 | loop fusion | flops 7077888 | bytes 7078656 | tf_op jit(solution)/shard_map/convert_element_type | solution.py:86
  48.8 4.3 %copy.102 = bf16[256,4608]{1,0:T(8,128)(2,1)} copy(bf16[256,4608]{0,1:T(8,128)(2,1)} %bitcast.314) | data formatting | bytes 4718592 | tf_op jit(solution)/shard_map/dot_general | solution.py:109
  53.7 36.1 %reduce-scatter.2.cloned.1.call-done = bf16[2,8,3,4608]{3,1,2,0:T(8,128)(2,1)} async-done(((bf16[16,8,3,4608]{3,1,2,0:T(8,128)(2,1)}), bf16[2,8,3,4608]{3,1,2,0:T(8,128)(2,1)}) %reduce-scatter.2.cloned.1.call-update) | async-done | bytes 442384 | tf_op jit(solution)/shard_map/reduce_scatter | solution.py:85
  89.8 1.8 copy.82
  92.1 47.6 %all-reduce.13.cloned.1.call-done = bf16[2,8,3,4608]{3,1,0,2:T(8,128)(2,1)} async-done(((bf16[2,8,3,4608]{3,1,0,2:T(8,128)(2,1)}), bf16[2,8,3,4608]{3,1,0,2:T(8,128)(2,1)}) %all-reduce.13.cloned.1.call-update) | async-done | bytes 442384 | tf_op jit(solution)/shard_map/psum | solution.py:88
  141.1 1.6 fusion.45
  142.7 1.7 fusion.48
  151.1 1.2 fusion.70
  152.4 1.2 fusion.69
  153.7 50.5 %all-reduce.15.cloned.1.call-done = (f32[16,4608]{1,0:T(8,128)}, f32[16,4608]{1,0:T(8,128)}, f32[16,4608]{1,0:T(8,128)}) async-done(((f32[16,4608]{1,0:T(8,128)}, f32[16,4608]{1,0:T(8,128)}, f32[16,4608]{1,0:T(8,128)}), (f32[16,4608]{1,0:T(8,128)}, f32[16,4608]{1,0:T(8,128)}, f32[16,4608]{1,0:T(8,128)})) %all-reduce.15.cloned.1.call-update) | async-done | bytes 884752 | tf_op jit(solution)/shard_map/psum | solution.py:135
  207.7 1.5 multiply_reduce_fusion.4
  211.5 14.2 %all_gather.19 = s32[3,16,8]{2,0,1:T(4,128)S(1)} all-gather(s32[3,2,8]{2,0,1:T(4,128)S(1)} %copy.92), channel_id=1, replica_groups=mesh['batch'=8,'vocab'=4] {'batch'}, dimensions={1}, use_global_device_ids=true | all-gather | bytes 1728 | tf_op jit(solution)/shard_map/all_gather | solution.py:77
  227.3 5.9 %all-gather.4.cloned.1.call-done = bf16[128,4608]{1,0:T(8,128)(2,1)} async-done(((bf16[16,4608]{1,0:T(8,128)(2,1)}), bf16[128,4608]{1,0:T(8,128)(2,1)}) %all-gather.4.cloned.1.call-update) | async-done | bytes 1179664 | tf_op jit(solution)/shard_map/all_gather | solution.py:140
  233.2 4.5 %select_reduce_fusion.2 = (f32[128]{0:T(128)S(1)}, f32[128]{0:T(128)S(1)}, f32[128]{0:T(128)S(1)}) fusion(s32[128]{0:T(128)S(1)} %sub.79, bf16[128,4608]{1,0:T(8,128)(2,1)} %all-gather.4.cloned.1.call-done, bf16[512,4608]{1,0:T(8,128)(2,1)} %param.20), kind=kOutput, calls=%fused_computation.103 | convolution fusion | flops 604438144 | bytes 5900288 | tf_op jit(solution)/shard_map/dot_general | solution.py:139
  237.7 19.4 %all-gather.6.cloned.1.call-done = bf16[128,4608]{1,0:T(8,128)(2,1)} async-done(((bf16[16,4608]{1,0:T(8,128)(2,1)}), bf16[128,4608]{1,0:T(8,128)(2,1)}) %all-gather.6.cloned.1.call-update) | async-done | bytes 1179664 | tf_op jit(solution)/shard_map/all_gather | solution.py:140
  257.1 4.5 %select_reduce_fusion.1 = (f32[128]{0:T(128)S(1)}, f32[128]{0:T(128)S(1)}, f32[128]{0:T(128)S(1)}) fusion(s32[128]{0:T(128)S(1)} %sub.82, bf16[128,4608]{1,0:T(8,128)(2,1)} %all-gather.6.cloned.1.call-done, bf16[512,4608]{1,0:T(8,128)(2,1)} %param.20), kind=kOutput, calls=%fused_computation.101 | convolution fusion | flops 604438144 | bytes 5900288 | tf_op jit(solution)/shard_map/dot_general | solution.py:139
  261.6 19.5 %all-gather.8.cloned.1.call-done = bf16[128,4608]{1,0:T(8,128)(2,1)} async-done(((bf16[16,4608]{1,0:T(8,128)(2,1)}), bf16[128,4608]{1,0:T(8,128)(2,1)}) %all-gather.8.cloned.1.call-update) | async-done | bytes 1179664 | tf_op jit(solution)/shard_map/all_gather | solution.py:140
  281.0 4.5 %select_reduce_fusion = (f32[128]{0:T(128)S(1)}, f32[128]{0:T(128)S(1)}, f32[128]{0:T(128)S(1)}) fusion(s32[128]{0:T(128)S(1)} %sub.85, bf16[128,4608]{1,0:T(8,128)(2,1)} %all-gather.8.cloned.1.call-done, bf16[512,4608]{1,0:T(8,128)(2,1)} %param.20), kind=kOutput, calls=%fused_computation.99 | convolution fusion | flops 604438144 | bytes 5900288 | tf_op jit(solution)/shard_map/dot_general | solution.py:139
  285.5 12.1 %all-reduce.7 = (f32[128]{0:T(128)S(1)}, f32[128]{0:T(128)S(1)}, f32[128]{0:T(128)S(1)}, f32[128]{0:T(128)S(1)}, f32[128]{0:T(128)S(1)}, /*index=5*/f32[128]{0:T(128)S(1)}) all-reduce(f32[128]{0:T(128)S(1)} %get-tuple-element.17, f32[128]{0:T(128)S(1)} %get-tuple-element.14, ...), channel_id=5, replica_groups=mesh['batch'=8,'vocab'=4] {'batch'}, use_global_device_ids=true, to_apply=%region_24.25.clone | all-reduce | flops 768 | bytes 6144
  298.1 8.0 %all-reduce.8 = (f32[16]{0:T(128)S(1)}, f32[16]{0:T(128)S(1)}, f32[16]{0:T(128)S(1)}, f32[16]{0:T(128)S(1)}, f32[16]{0:T(128)S(1)}, /*index=5*/f32[16]{0:T(128)S(1)}) all-reduce(f32[16]{0:T(128)S(1)} %dynamic-slice.5, f32[16]{0:T(128)S(1)} %dynamic-slice.3, f32[16]{0:T(128)S(1)} %dynamic-slice.1, ...), channel_id=1, replica_groups=mesh['batch'=8,'vocab'=4] {'vocab'}, use_global_device_ids=true, to_apply=%region_25.26 | all-reduce | flops 96 | bytes 768 | tf_op jit(solution)/shard_map/psum | solution.py:156
  306.4 44.3 %all-reduce.6 = (f32[128]{0:T(128)S(1)}, f32[128]{0:T(128)S(1)}, f32[128]{0:T(128)S(1)}) all-reduce(f32[128]{0:T(128)S(1)} %get-tuple-element.16, f32[128]{0:T(128)S(1)} %get-tuple-element.13, f32[128]{0:T(128)S(1)} %get-tuple-element.10), channel_id=1, replica_groups=mesh['batch'=8,'vocab'=4] {'batch','vocab'}, use_global_device_ids=true, to_apply=%region_31.32 | all-reduce | flops 384 | bytes 3072 | tf_op jit(solution)/shard_map/pmax | solution.py:157
  (131 shorter events, 20.4 us)
Async XLA Ops:
  7.2 142.7 %copy-start = (bf16[256,4608]{1,0:T(8,128)(2,1)S(1)}, bf16[256,4608]{1,0:T(8,128)(2,1)}, u32[]{:S(2)}) copy-start(bf16[256,4608]{1,0:T(8,128)(2,1)} %param.27) | copy-start | bytes 7077892
  7.2 82.6 %reduce-scatter.2.cloned.1.call-start = ((), (), s32[]{:S(2)}) async-start(), calls=%async_computation.1 | async-start | bytes 3981312 | tf_op jit(solution)/shard_map/reduce_scatter | solution.py:85
  48.7 90.9 %all-reduce.13.cloned.1.call-start = ((), (), s32[]{:S(2)}) async-start(), calls=%async_computation.2 | async-start | bytes 884736 | tf_op jit(solution)/shard_map/psum | solution.py:88
  48.8 4.4 %copy-start.14 = (s32[2]{0:T(128)S(1)}, s32[2]{0:T(128)}, u32[]{:S(2)}) copy-start(s32[2]{0:T(128)} %param.19) | copy-start | bytes 28
  48.8 4.5 %copy-start.12 = (s32[2,2]{1,0:T(2,128)S(1)}, s32[2,2]{1,0:T(2,128)}, u32[]{:S(2)}) copy-start(s32[2,2]{1,0:T(2,128)} %param.17) | copy-start | bytes 52
  48.8 4.5 %copy-start.13 = (s32[2,2]{1,0:T(2,128)S(1)}, s32[2,2]{1,0:T(2,128)}, u32[]{:S(2)}) copy-start(s32[2,2]{1,0:T(2,128)} %param.18) | copy-start | bytes 52
  53.2 87.9 %copy-start.4 = (f32[4608]{0:T(1024)S(1)}, f32[4608]{0:T(1024)}, u32[]{:S(2)}) copy-start(f32[4608]{0:T(1024)} %param.21) | copy-start | bytes 55300
  91.6 112.6 %all-reduce.15.cloned.1.call-start = ((), (), s32[]{:S(2)}) async-start(), calls=%async_computation.6 | async-start | bytes 1769472 | tf_op jit(solution)/shard_map/psum | solution.py:135
  139.7 4.7 %copy-start.3 = (bf16[4608,128]{1,0:T(8,128)(2,1)S(1)}, bf16[4608,128]{1,0:T(8,128)(2,1)}, u32[]{:S(2)}) copy-start(bf16[4608,128]{1,0:T(8,128)(2,1)} %param.26) | copy-start | bytes 3538948
  142.6 2.4 copy-start.2
  144.7 1.7 copy-start.1
  147.1 1.7 copy-start.15
  147.8 2.1 copy-start.8
  152.4 55.3 %copy-start.9 = (f32[4608]{0:T(1024)S(1)}, f32[4608]{0:T(1024)}, u32[]{:S(2)}) copy-start(f32[4608]{0:T(1024)} %param.22) | copy-start | bytes 55300
  153.6 55.6 %copy-start.10 = (f32[4608]{0:T(1024)S(1)}, f32[4608]{0:T(1024)}, u32[]{:S(2)}) copy-start(f32[4608]{0:T(1024)} %param.23) | copy-start | bytes 55300
  153.6 79.6 %all-gather.4.cloned.1.call-start = ((), (), s32[]{:S(2)}) async-start(), calls=%async_computation.3 | async-start | bytes 1327104 | tf_op jit(solution)/shard_map/all_gather | solution.py:140
  204.2 5.1 %copy-start.5 = (f32[16,4608]{1,0:T(8,128)S(1)}, f32[16,4608]{1,0:T(8,128)}, u32[]{:S(2)}) copy-start(f32[16,4608]{1,0:T(8,128)} %get-tuple-element.36) | copy-start | bytes 884740
  204.2 5.1 %copy-start.6 = (f32[16,4608]{1,0:T(8,128)S(1)}, f32[16,4608]{1,0:T(8,128)}, u32[]{:S(2)}) copy-start(f32[16,4608]{1,0:T(8,128)} %get-tuple-element.37) | copy-start | bytes 884740
  204.2 5.1 %copy-start.7 = (f32[16,4608]{1,0:T(8,128)S(1)}, f32[16,4608]{1,0:T(8,128)}, u32[]{:S(2)}) copy-start(f32[16,4608]{1,0:T(8,128)} %get-tuple-element.38) | copy-start | bytes 884740
  206.5 4.9 %copy-start.11 = (s32[3,2,8]{2,1,0:T(2,128)S(1)}, s32[3,2,8]{2,1,0:T(2,128)}, u32[]{:S(2)}) copy-start(s32[3,2,8]{2,1,0:T(2,128)} %param.16) | copy-start | bytes 580
  207.6 18.4 %copy-start.16 = (u32[32]{0:T(128)S(1)}, u32[32]{0:T(128)}, u32[]{:S(2)}) copy-start(u32[32]{0:T(128)} %constant.94) | copy-start | bytes 388
  210.3 46.8 %all-gather.6.cloned.1.call-start = ((), (), s32[]{:S(2)}) async-start(), calls=%async_computation.4 | async-start | bytes 1327104 | tf_op jit(solution)/shard_map/all_gather | solution.py:140
  210.9 70.2 %all-gather.8.cloned.1.call-start = ((), (), s32[]{:S(2)}) async-start(), calls=%async_computation.5 | async-start | bytes 1327104 | tf_op jit(solution)/shard_map/all_gather | solution.py:140
Sparse Core Ops, SparseCore 0:
  48.9 40.8 reduce-scatter.1
  92.8 46.8 all-reduce.12
  153.7 50.3 all-reduce.14
  210.4 22.7 all-gather.3
  234.7 22.3 all-gather.5
  258.6 22.4 all-gather.7
where the time goes:
time: 361 us; the launch traced here: 360 us
  waiting for transfers between devices  180 us (50%)
  blocking collectives  92.9 us (26%)
  local copies, waits for them, and re-layouts  30 us (8%)
  matrix products  24.9 us (7%)
  other arithmetic  16.6 us (5%)
  between operations  15.1 us (4%)
    psum x1, waiting for transfers between devices, per_device(): whole_branch = lax.psum(branch, 'vocab')  50.5 us
    psum x1, waiting for transfers between devices, per_device(): embedded_all = lax.psum(column_rows, 'vocab').astype(jnp.float32)  47.6 us
    all_gather x3, waiting for transfers between devices, per_device(): lax.all_gather(final_rows, 'batch', axis=0, tiled=True)  44.7 us
    pmax x1, blocking collectives, per_device(): tops_joint = lax.pmax(largest, ('batch', 'vocab'))  44.3 us
    reduce_scatter x1, waiting for transfers between devices, per_device(): lax.psum_scatter(lookup_terms.astype(jnp.bfloat16), 'batch', scatter_dime...  36.1 us
    gather x2, local copies, waits for them, and re-layouts, per_device(): looked_up = jnp.take(table, jnp.clip(ordered, 0, vocab_rows - 1), axis=0)  19.4 us
    all_gather x1, blocking collectives, per_device(): lax.all_gather(window_ids, 'batch', axis=1, tiled=True)  14.3 us
    all_gather x1, blocking collectives, per_device(): lax.all_gather(pool_ids, 'batch', axis=1, tiled=True)  14.2 us
  transfers between devices with their start and end apart: 6, of which 6 were waited for; matrix products, arithmetic and copies ran while one was open for 4% of the time, Pallas kernels for 0%

commit v1 on v0

v1 whole, which is shorter than its diff:
```python
import functools
import math

import jax
import jax.numpy as jnp
import numpy as np
from jax import lax
from jax.experimental import pallas as pl
from jax.experimental.pallas import tpu as pltpu
from jax.sharding import PartitionSpec as P


epsilon = 1e-06
query_scalar = 144.0
score_cap = 50.0
logit_cap = 30.0
slots_sent = 12
half_count = 2
lane_count = 128


f32 = jnp.float32
bf16 = jnp.bfloat16
smem = pl.BlockSpec(memory_space=pltpu.SMEM)
vmem = pl.BlockSpec(memory_space=pltpu.VMEM)


def normalize(values_in, gain):
    return (
        values_in
        * lax.rsqrt(jnp.mean(values_in * values_in, axis=-1, keepdims=True) + epsilon)
        * gain
    )


def bits_of(size):
    return [1 << place for place in range(size.bit_length() - 1)]


def iota(shape, dimension):
    return lax.broadcasted_iota(jnp.int32, shape, dimension)


def owner_of(order, at_vocab, at_core):
    vocab_bits = bits_of(lax.axis_size("vocab"))
    last = len(vocab_bits) - 1
    total = order ^ order
    for step in range(len(vocab_bits)):
        bit = jnp.where(at_core == 0, vocab_bits[step], vocab_bits[last - step])
        total = total ^ (((order >> (last - step)) & 1) * bit)
    return total ^ at_vocab


def side_by_side(ref, first, count, found, stride):
    parts = [ref[pl.ds(first + at, found, stride=stride), :] for at in range(count)]
    return jnp.concatenate(parts, axis=1)


def slot_hits(ids, first, extent, first_slot):
    size = ids.shape[-1]
    inside = (ids >= first) & (ids < first + extent)
    before = iota((size, size), 0) < iota((size, size), 1)
    rank = jnp.dot(
        jnp.broadcast_to(jnp.where(inside, 1.0, 0.0), (8, size)),
        jnp.where(before, 1.0, 0.0),
        preferred_element_type=f32,
    )[:1]
    slots = iota((half_count * slots_sent, size), 0) % slots_sent + first_slot
    return (rank == slots.astype(f32)) & inside


def of_chip(ids, at, at_core):
    mine, other = ids[at : at + 1, :], ids[at + 1 : at + 2, :]
    first = jnp.where(at_core == 0, mine, other)
    second = jnp.where(at_core == 0, other, mine)
    return jnp.concatenate([first, second], axis=1)


def pack_kernel(windows, pools, ids, held, done):
    copies = [
        pltpu.make_async_copy(ref, held.at[at], done.at[at])
        for at, ref in enumerate((windows, pools))
    ]
    for copy in copies:
        copy.start()
    for copy in copies:
        copy.wait()
    groups = windows.shape[0] * windows.shape[1]
    for kind in range(2):
        for at in range(windows.shape[0]):
            first = kind * groups + at * windows.shape[1]
            ids[first : first + windows.shape[1], :] = held[kind, at]


def send_kernel(first_slot, ids, table, *outs):
    batch_devices = lax.axis_size("batch")
    vocab_devices = lax.axis_size("vocab")
    far = batch_devices // 2
    at_core = lax.axis_index("batch") % 2
    vocab_rows, model_width = table.shape
    first = (lax.axis_index("batch") * vocab_devices + lax.axis_index("vocab")) * vocab_rows
    sent, pools, most = outs[:far], outs[far], outs[far + 1]
    stride = ids.shape[0] // batch_devices
    tokens = side_by_side(ids, 0, stride // 2, batch_devices, stride)
    pools[...] = side_by_side(ids, stride // 2, stride // 2, batch_devices, stride)
    block = half_count * slots_sent
    lanes = iota((block, vocab_rows), 1)
    one_hots = []
    for at in range(far):
        at_ids = of_chip(tokens, 2 * at, at_core)
        hits = slot_hits(at_ids, first, vocab_rows, first_slot[0])
        picked = jnp.sum(
            jnp.where(hits, (at_ids - first + 1).astype(f32), 0.0), axis=1, keepdims=True
        )
        one_hots.append(jnp.where(picked.astype(jnp.int32) - 1 == lanes, 1.0, 0.0).astype(f32))
    one_hot = jnp.concatenate(one_hots, axis=0)
    half_of = (iota(one_hot.shape, 0) % block) // slots_sent
    wide = model_width // half_count
    rows = jnp.zeros((one_hot.shape[0], wide), f32)
    for half in range(half_count):
        rows = rows + jnp.dot(
            jnp.where(half_of == half, one_hot, 0.0).astype(bf16),
            table[:, half * wide : (half + 1) * wide],
            preferred_element_type=f32,
        )
    for at in range(far):
        sent[at][...] = rows[at * block : (at + 1) * block].astype(bf16)
    owner = lax.div(tokens, jnp.full_like(tokens, vocab_rows)).astype(f32)
    columns = jnp.transpose(owner)
    largest = jnp.zeros((1, owner.shape[1]), f32)
    for at in range(batch_devices):
        equal = jnp.zeros((owner.shape[1], owner.shape[1]), f32)
        for other in (at, at ^ 1):
            equal = equal + jnp.where(
                columns[:, other : other + 1] == owner[at : at + 1, :], 1.0, 0.0
            )
        largest = jnp.maximum(largest, jnp.sum(equal, axis=0, keepdims=True))
    most[0] = jnp.max(largest).astype(jnp.int32)


def place_kernel(first_slot, vocab_rows, ids, *refs):
    parts, placed = refs[:-half_count], refs[-half_count:]
    batch_devices = lax.axis_size("batch")
    at_core = lax.axis_index("batch") % 2
    stride = ids.shape[0] // batch_devices
    tokens = side_by_side(ids, 0, stride // 2, 2, stride)
    size = tokens.shape[1]
    chip = of_chip(tokens, 0, at_core)
    hits = []
    for at in range(len(parts)):
        other = at // (batch_devices // 2)
        relative = 2 * (at % (batch_devices // 2)) + other
        source = (lax.axis_index("batch") ^ relative) * lax.axis_size("vocab")
        first = (source + lax.axis_index("vocab")) * vocab_rows
        found = jnp.where(slot_hits(chip, first, vocab_rows, first_slot[0]), 1.0, 0.0)
        hits.append(jnp.where(at_core == 0, found[:, :size], found[:, size:]))
    hits = jnp.concatenate(hits, axis=0)
    half_of = (iota(hits.shape, 0) % (half_count * slots_sent)) // slots_sent
    values = jnp.concatenate([part[...].astype(f32) for part in parts], axis=0).astype(bf16)
    for half in range(half_count):
        placed[half][...] = lax.dot_general(
            jnp.where(half_of == half, hits, 0.0).astype(bf16),
            values,
            (((0,), (0,)), ((), ())),
            preferred_element_type=f32,
        ).astype(bf16)


def turn_kernel(accepted, converged, cache_lens, freqs, signs, cosine, sine):
    windows = accepted.shape[0] + 1
    width = cosine.shape[0] // (windows * cache_lens.shape[0])
    positions = []
    for at in range(windows):
        for at_batch in range(cache_lens.shape[0]):
            start = cache_lens[at_batch]
            for before in range(at):
                start = start + jnp.where(
                    converged[before, at_batch] == 1, width, accepted[before, at_batch]
                )
            positions.append(iota((width, cosine.shape[1]), 0) + start)
    angles = jnp.concatenate(positions, axis=0).astype(f32) * freqs[...]
    cosine[...] = jnp.cos(angles)
    sine[...] = jnp.sin(angles) * signs[...]


def attend_kernel(
    accepted,
    converged,
    cache_lens,
    kept_first,
    kept_second,
    got_first,
    got_second,
    cosine,
    sine,
    attn_gain,
    w_query,
    w_key,
    w_value,
    w_out,
    cache_keys,
    cache_values,
    keep,
    send,
    own,
):
    rows = got_first.shape[0]
    model_width = w_query.shape[0]
    local_batch, kv_local, cache_slots, head_size = cache_keys.shape
    iter_count = accepted.shape[0] + 1
    width = rows // (iter_count * local_batch)
    tokens = iter_count * width
    chunk = own.shape[0]
    at_vocab = lax.axis_index("vocab")
    at_core = lax.axis_index("batch") % 2
    gathered = jnp.concatenate(
        [
            kept_first[...].astype(f32) + got_first[...].astype(f32),
            kept_second[...].astype(f32) + got_second[...].astype(f32),
        ],
        axis=1,
    )
    embedded = gathered * math.sqrt(model_width)
    normed = normalize(embedded, attn_gain[...]).astype(bf16)

    def turned(values):
        return values * cosine[...] + pltpu.roll(values, head_size // 2, 1) * sine[...]

    queries = jnp.dot(normed, w_query[...], preferred_element_type=f32)
    keys = jnp.dot(normed, w_key[...], preferred_element_type=f32)
    values = jnp.dot(normed, w_value[...], preferred_element_type=f32)

    def of_sequence(array, at_batch, head):
        starts = [(at * local_batch + at_batch) * width for at in range(iter_count)]
        lanes = slice(head * head_size, (head + 1) * head_size)
        return jnp.concatenate([array[at : at + width, lanes] for at in starts], axis=0)

    nt = (((1,), (1,)), ((), ()))
    attended_rows = []
    turned_queries = [
        turned(queries[:, head * head_size : (head + 1) * head_size]) / math.sqrt(query_scalar)
        for head in range(2 * kv_local)
    ]
    turned_keys = [
        turned(keys[:, head * head_size : (head + 1) * head_size]) for head in range(kv_local)
    ]
    for at_batch in range(local_batch):
        taken = [
            jnp.where(converged[at, at_batch] == 1, width, accepted[at, at_batch])
            for at in range(iter_count - 1)
        ]
        query_at = iota((2 * tokens, tokens), 0) % tokens
        key_at = iota((2 * tokens, tokens), 1)
        key_taken = jnp.zeros((2 * tokens, tokens), jnp.int32)
        for at in range(iter_count - 1):
            key_taken = jnp.where(key_at // width == at, taken[at], key_taken)
        earlier = (key_at // width < query_at // width) & (key_at % width < key_taken)
        same = (key_at // width == query_at // width) & (key_at <= query_at)
        visible_now = earlier | same
        visible_cache = iota((2 * tokens, cache_slots), 1) < cache_lens[at_batch]
        heads = []
        for head in range(kv_local):
            pair = jnp.concatenate(
                [
                    of_sequence(turned_queries[2 * head], at_batch, 0),
                    of_sequence(turned_queries[2 * head + 1], at_batch, 0),
                ],
                axis=0,
            ).astype(bf16)
            keys_now = of_sequence(turned_keys[head], at_batch, 0).astype(bf16)
            values_now = of_sequence(values, at_batch, head).astype(bf16)

            def weigh(scores, visible):
                scores = score_cap * jnp.tanh(scores / score_cap)
                return jnp.where(visible, jnp.exp(scores), 0.0)

            from_cache = weigh(
                lax.dot_general(pair, cache_keys[at_batch, head], nt, preferred_element_type=f32),
                visible_cache,
            )
            from_now = weigh(
                lax.dot_general(pair, keys_now, nt, preferred_element_type=f32), visible_now
            )
            weight_sum = jnp.sum(from_cache, axis=1, keepdims=True) + jnp.sum(
                from_now, axis=1, keepdims=True
            )
            summed = jnp.dot(
                from_cache.astype(bf16), cache_values[at_batch, head], preferred_element_type=f32
            ) + jnp.dot(from_now.astype(bf16), values_now, preferred_element_type=f32)
            attended = summed / weight_sum
            heads += [attended[:tokens], attended[tokens:]]
        attended_rows.append(jnp.concatenate(heads, axis=1))
    attended = jnp.concatenate(attended_rows, axis=0).astype(bf16)

    ordered = iota((rows, rows), 0)
    wanted = owner_of(ordered // chunk, at_vocab, at_core) * chunk + ordered % chunk
    place = iota((rows, rows), 1)
    at_batch = place // tokens
    at_window = (place % tokens) // width
    standing = (at_window * local_batch + at_batch) * width + place % width
    by_sequence = jnp.where(wanted == standing, 1.0, 0.0).astype(bf16)
    by_window = jnp.where(wanted == place, 1.0, 0.0)[:chunk].astype(bf16)
    own[...] = jnp.dot(by_window, gathered.astype(bf16), preferred_element_type=f32).astype(bf16)
    attended = jnp.dot(by_sequence, attended, preferred_element_type=f32).astype(bf16)
    half = rows // 2
    send[...] = jnp.dot(attended[half:], w_out[...], preferred_element_type=f32).astype(bf16)
    keep[...] = jnp.dot(attended[:half], w_out[...], preferred_element_type=f32)


def halve_kernel(kept, got, keep, send):
    half = keep.shape[0]
    total = kept[...] + got[...].astype(f32)
    keep[...] = total[:half]
    send[...] = total[half:].astype(bf16)


def final_kernel(kept, got, own, post_gain, final_gain, final):
    model_width = kept.shape[1]
    branch = kept[...] + got[...].astype(f32)
    embedded = own[...].astype(f32) * math.sqrt(model_width)
    hidden = embedded + normalize(branch, post_gain[...])
    rows = normalize(hidden, final_gain[...])
    wide = model_width // half_count
    final[...] = jnp.concatenate(
        [rows[:, half * wide : (half + 1) * wide] for half in range(half_count)], axis=0
    ).astype(bf16)


def assemble_kernel(*refs):
    parts, block = refs[:-1], refs[-1]
    wide = parts[0].shape[1]
    chunk = parts[0].shape[0] // half_count
    values = [part[...].astype(f32) for part in parts]
    for half in range(half_count):
        block[:, half * wide : (half + 1) * wide] = jnp.concatenate(
            [value[half * chunk : (half + 1) * chunk] for value in values], axis=0
        ).astype(bf16)


def score_blocks(blocks, core_of, order_of, tables, pools):
    vocab_rows = sum(table.shape[0] for table in tables)
    vocab_devices = lax.axis_size("vocab")
    at_vocab = lax.axis_index("vocab")
    at_core = lax.axis_index("batch") % 2
    far = lax.axis_size("batch") // 2
    block_rows = blocks[0][0].shape[0]
    chunk = block_rows // far
    first = (lax.axis_index("batch") * vocab_devices + at_vocab) * vocab_rows
    wanted = []
    for other, order in zip(core_of, order_of):
        owner = owner_of(jnp.int32(order), at_vocab, at_core ^ other)
        parts = []
        for at in range(far):
            pool = pools[2 * at + other : 2 * at + other + 1, :]
            part = jnp.zeros((1, chunk), jnp.int32)
            for place in range(vocab_devices):
                part = jnp.where(
                    owner == place, pool[:, place * chunk : (place + 1) * chunk], part
                )
            parts.append(part)
        wanted.append(jnp.concatenate(parts, axis=1))
    wanted = jnp.concatenate(wanted, axis=1) - first
    values = [
        jnp.concatenate([block[half][...] for block in blocks], axis=0)
        for half in range(len(blocks[0]))
    ]
    wide = values[0].shape[1]
    sums, chosen, largest = [], [], []
    for table in tables:
        raw = jnp.zeros((table.shape[0], values[0].shape[0]), f32)
        for half, value in enumerate(values):
            raw = raw + lax.dot_general(
                table[:, half * wide : (half + 1) * wide],
                value,
                (((1,), (1,)), ((), ())),
                preferred_element_type=f32,
            )
        logits = logit_cap * jnp.tanh(raw / logit_cap)
        sums.append(jnp.sum(jnp.exp(logits), axis=0, keepdims=True))
        hit = iota(logits.shape, 0) == wanted
        chosen.append(jnp.sum(jnp.where(hit, logits, 0.0), axis=0, keepdims=True))
        largest.append(jnp.max(logits, axis=0, keepdims=True))
        wanted = wanted - table.shape[0]
    sums, chosen = sum(sums), sum(chosen)
    top = largest[0]
    for row in largest[1:]:
        top = jnp.maximum(top, row)
    largest = top
    return [
        [row[:, at * block_rows : (at + 1) * block_rows] for at in range(len(blocks))]
        for row in (sums, chosen, largest)
    ]


def score_kernel(orders, halves, parts, *refs):
    pools, scores = refs[-2:]
    tables = refs[len(refs) - 2 - parts : -2]
    blocks = [refs[at * halves : (at + 1) * halves] for at in range(2 * len(orders))]
    found = score_blocks(blocks, [0] * len(orders) + [1] * len(orders), orders * 2, tables, pools)
    for kind in range(3):
        for at in range(len(blocks)):
            row = kind * len(blocks) + at
            scores[row : row + 1, :] = found[kind][at]


def late_kernel(orders, halves, parts, *refs):
    vocab_devices = lax.axis_size("vocab")
    at_vocab = lax.axis_index("vocab")
    at_batch = lax.axis_index("batch")
    far = lax.axis_size("batch") // 2
    message = refs[-1]
    scores = refs[-1 - len(orders) : -1]
    pools = refs[-2 - len(orders)]
    tables = refs[2 * halves : 2 * halves + parts]
    blocks = [refs[:halves], refs[halves : 2 * halves]]
    block_rows = blocks[0][0].shape[0]
    chunk = block_rows // far
    late = score_blocks(blocks, [0, 1], [vocab_devices - 1] * 2, tables, pools)
    for other in range(2):
        kinds = []
        for kind in range(3):
            found = []
            for group, score in zip(orders, scores):
                row = (kind * 2 + other) * len(group)
                found += [score[row + at : row + at + 1, :] for at in range(len(group))]
            found.append(late[kind][other])
            owners = [
                owner_of(jnp.int32(at), at_vocab, (at_batch % 2) ^ other)
                for at in range(vocab_devices)
            ]
            chunks = []
            for place in range(vocab_devices):
                total = jnp.zeros_like(found[0])
                for at in range(vocab_devices):
                    total = jnp.where(owners[at] == place, found[at], total)
                chunks.append(total)
            kinds.append(jnp.concatenate(chunks, axis=0))
        for at in range(far):
            pieces = [kind[:, at * chunk : (at + 1) * chunk] for kind in kinds]
            pieces.append(jnp.zeros((vocab_devices, lane_count - 3 * chunk), f32))
            piece = jnp.concatenate(pieces, axis=1)
            piece = jnp.concatenate([piece] * vocab_devices, axis=0)
            target = at_batch ^ (2 * at + other)
            size = vocab_devices * vocab_devices
            message[pl.ds(pl.multiple_of(target * size, 8), size), :] = piece


def result_kernel(got, log_total, best_logit, pool_score):
    vocab_devices = lax.axis_size("vocab")
    iter_count, local_batch, width = log_total.shape
    rows = iter_count * local_batch * width
    chunk = rows // vocab_devices
    step = max(8, vocab_devices)
    added = got[0:step, :]
    largest = added
    for at in range(1, got.shape[0] // step):
        part = got[at * step : (at + 1) * step, :]
        added = added + part
        largest = jnp.maximum(largest, part)
    total, top = added[:vocab_devices], largest[:vocab_devices]
    for at in range(1, step // vocab_devices):
        total = total + added[at * vocab_devices : (at + 1) * vocab_devices]
        top = jnp.maximum(top, largest[at * vocab_devices : (at + 1) * vocab_devices])

    def flat(array, kind):
        return jnp.concatenate(
            [array[at : at + 1, kind * chunk : (kind + 1) * chunk] for at in range(vocab_devices)],
            axis=1,
        )

    log_sum = jnp.log(flat(total, 0))
    for ref, found in (
        (log_total, log_sum),
        (best_logit, flat(top, 2)),
        (pool_score, flat(total, 1) - log_sum),
    ):
        for at in range(iter_count):
            for at_batch in range(local_batch):
                start = (at * local_batch + at_batch) * width
                ref[at, at_batch : at_batch + 1, :] = found[:, start : start + width]


def call(kernel, shapes, in_specs, out_specs, flops=0, scratch=(), grant=8):
    return pl.pallas_call(
        kernel,
        out_shape=shapes,
        in_specs=in_specs,
        out_specs=out_specs,
        scratch_shapes=scratch,
        compiler_params=pltpu.CompilerParams(vmem_limit_bytes=grant << 20),
        cost_estimate=pl.CostEstimate(flops=flops, bytes_accessed=flops // 100, transcendentals=0),
    )


def per_device(
    window_ids,
    pool_ids,
    accepted,
    converged,
    cache_lens,
    table,
    attn_gain,
    post_gain,
    final_gain,
    w_query,
    w_key,
    w_value,
    w_out,
    cache_keys,
    cache_values,
):
    iter_count, local_batch, width = window_ids.shape
    vocab_rows, model_width = table.shape
    head_size = cache_keys.shape[3]
    groups = iter_count * local_batch
    rows = groups * width
    batch_devices = lax.axis_size("batch")
    vocab_devices = lax.axis_size("vocab")
    all_devices = batch_devices * vocab_devices
    vocab_bits = bits_of(vocab_devices)
    chunk = rows // vocab_devices
    far = batch_devices // 2

    def shape(*dims, kind=bf16):
        return jax.ShapeDtypeStruct(dims, kind)

    def batch_swap(value, mask):
        return lax.ppermute(value, "batch", [(at, at ^ mask) for at in range(batch_devices)])

    def mixed_swap(value, step):
        pairs = []
        for at in range(all_devices):
            b_at, v_at = divmod(at, vocab_devices)
            bit = vocab_bits[step] if b_at % 2 == 0 else vocab_bits[-1 - step]
            pairs.append((at, b_at * vocab_devices + (v_at ^ bit)))
        return lax.ppermute(value, ("batch", "vocab"), pairs)

    in_hbm = pl.BlockSpec(memory_space=pltpu.HBM)
    own_ids = call(
        pack_kernel,
        shape(2 * groups, width, kind=jnp.int32),
        [in_hbm] * 2,
        vmem,
        scratch=[
            pltpu.VMEM((2, iter_count, local_batch, width), jnp.int32),
            pltpu.SemaphoreType.DMA((2,)),
        ],
        grant=2,
    )(window_ids, pool_ids)
    all_ids = own_ids
    for bit in bits_of(batch_devices):
        all_ids = jnp.concatenate([all_ids, batch_swap(all_ids, bit)], axis=0)

    def exchange(first_slot):
        *sent, pools, most = call(
            send_kernel,
            [shape(half_count * slots_sent, model_width // half_count)] * far
            + [shape(batch_devices, rows, kind=jnp.int32), shape(1, kind=jnp.int32)],
            [smem, vmem, vmem],
            [vmem] * (far + 1) + [smem],
            flops=2 * batch_devices * slots_sent * vocab_rows * model_width,
            grant=10,
        )(first_slot, all_ids, table)
        got = [sent[0]]
        for mask in range(1, far):
            got.append(batch_swap(sent[mask], 2 * mask))
        other = [batch_swap(part, 1) for part in got]
        placed = call(
            lambda slot, *refs: place_kernel(slot, vocab_rows, *refs),
            [shape(rows, model_width // half_count)] * half_count,
            [smem, vmem] + [vmem] * batch_devices,
            [vmem] * half_count,
            flops=10**8,
        )(first_slot, all_ids, *got, *other)
        return placed, pools, most

    start_slot = jnp.zeros((1,), jnp.int32)
    gathered, pools, most = exchange(start_slot)

    def another_round(state):
        later = state[0] + slots_sent
        return later, [old + new for old, new in zip(state[1], exchange(later)[0])]

    _, gathered = lax.while_loop(
        lambda state: state[0][0] + slots_sent < most[0], another_round, (start_slot, list(gathered))
    )
    for step in range(len(vocab_bits) - 1):
        received = []
        for half in range(half_count):
            received.append(mixed_swap(gathered[half], step))
        gathered = [kept + got for kept, got in zip(gathered, received)]
    received = []
    for half in range(half_count):
        received.append(mixed_swap(gathered[half], len(vocab_bits) - 1))

    half_size = head_size // 2
    freqs = np.float32(10000.0) ** (-np.arange(half_size, dtype=np.float32) / half_size)
    signs = np.concatenate([-np.ones(half_size), np.ones(half_size)]).astype(np.float32)
    cosine, sine = call(
        turn_kernel,
        [shape(rows, head_size, kind=f32)] * 2,
        [smem] * 3 + [vmem] * 2,
        [vmem] * 2,
        flops=10**7,
    )(
        accepted,
        converged,
        cache_lens,
        jnp.asarray(np.concatenate([freqs, freqs])[None]),
        jnp.asarray(signs[None]),
    )

    wide = w_query.shape[1] + w_key.shape[1] + w_value.shape[1]
    keep, send, own = call(
        attend_kernel,
        [
            shape(rows // 2, model_width, kind=f32),
            shape(rows // 2, model_width),
            shape(chunk, model_width),
        ],
        [smem] * 3 + [vmem] * 13,
        [vmem] * 3,
        flops=2 * rows * model_width * (wide + w_out.shape[0]),
        grant=20,
    )(
        accepted,
        converged,
        cache_lens,
        *gathered,
        *received,
        cosine,
        sine,
        attn_gain[None],
        w_query,
        w_key,
        w_value,
        w_out,
        cache_keys,
        cache_values,
    )
    for step in range(len(vocab_bits) - 1):
        half = keep.shape[0] // 2
        keep, send = call(
            halve_kernel,
            [shape(half, model_width, kind=f32), shape(half, model_width)],
            [vmem] * 2,
            [vmem] * 2,
        )(keep, mixed_swap(send, step))
    final = call(
        final_kernel,
        shape(half_count * chunk, model_width // half_count),
        [vmem] * 5,
        vmem,
    )(keep, mixed_swap(send, len(vocab_bits) - 1), own, post_gain[None], final_gain[None])

    parts = [final]
    for mask in range(1, far):
        parts.append(batch_swap(final, 2 * mask))
    blocks = [
        call(assemble_kernel, shape(far * chunk, model_width), [vmem] * far, vmem)(*parts)
    ]
    for step in range(len(vocab_bits)):
        step = len(vocab_bits) - 1 - step
        for at in range(len(blocks)):
            blocks.append(mixed_swap(blocks[at], step))
    halves = 1
    own_blocks = [blocks]
    other_blocks = [[batch_swap(each, 1) for each in blocks]]

    per_block = 2 * far * chunk * vocab_rows * model_width

    def halves_of(blocks, orders):
        return [blocks[half][order] for order in orders for half in range(halves)]

    groups_of = [[0], list(range(1, vocab_devices - 1))]
    scores = []
    for orders in groups_of:
        inputs = halves_of(own_blocks, orders) + halves_of(other_blocks, orders)
        scores.append(
            call(
                functools.partial(score_kernel, orders, halves, 1),
                shape(6 * len(orders), far * chunk, kind=f32),
                [vmem] * (len(inputs) + 1 + 1),
                vmem,
                flops=2 * per_block * len(orders),
            )(*inputs, table, pools)
        )
    last = [vocab_devices - 1]
    message = call(
        functools.partial(late_kernel, groups_of, halves, 1),
        shape(all_devices * vocab_devices, lane_count, kind=f32),
        [vmem] * (2 * halves + 1 + 1 + len(scores)),
        vmem,
        flops=2 * per_block,
    )(*halves_of(own_blocks, last), *halves_of(other_blocks, last), table, pools, *scores)
    totals = lax.all_to_all(message, ("batch", "vocab"), 0, 0, tiled=True)
    return tuple(
        call(
            result_kernel,
            [shape(iter_count, local_batch, width, kind=f32)] * 3,
            [vmem],
            [vmem] * 3,
        )(totals)
    )


def solution(mesh):
    return jax.shard_map(
        per_device,
        mesh=mesh,
        in_specs=(
            P(None, "batch", None),
            P(None, "batch", None),
            P(None, "batch"),
            P(None, "batch"),
            P("batch"),
            P(("batch", "vocab"), None),
            P(),
            P(),
            P(),
            P(None, "vocab"),
            P(None, "vocab"),
            P(None, "vocab"),
            P("vocab", None),
            P("batch", "vocab", None, None),
            P("batch", "vocab", None, None),
        ),
        out_specs=(P(None, "batch", None), P(None, "batch", None), P(None, "batch", None)),
        check_vma=False,
    )
```

time: 361 us -> 108 us (0.30)
  the two profiles are of different devices: /device:TPU:10 before, /device:TPU:0 now
where the time goes in v1:
time: 108 us
  waiting for transfers between devices  48.6 us (45%)
  starting transfers between devices  29.8 us (28%)
  Pallas kernels  14.1 us (13%)
  blocking collectives  12.1 us (11%)
  local copies, waits for them, and re-layouts  1.5 us (1%)
    ppermute x9, waiting for transfers between devices, mixed_swap(): return lax.ppermute(value, ('batch', 'vocab'), pairs)  31.5 us
    ppermute x17, waiting for transfers between devices, batch_swap(): lax.ppermute(value, 'batch', [(at, at ^ mask) for at in range(batch_devic...  17.1 us
    ppermute x17, starting transfers between devices, batch_swap(): lax.ppermute(value, 'batch', [(at, at ^ mask) for at in range(batch_devic...  16.8 us
    ppermute x9, starting transfers between devices, mixed_swap(): return lax.ppermute(value, ('batch', 'vocab'), pairs)  13 us
    all_to_all x1, blocking collectives, per_device(): totals = lax.all_to_all(message, ('batch', 'vocab'), 0, 0, tiled=True)  12.1 us
    pallas_call x1, Pallas kernels, exchange(): call(send_kernel, [shape(half_count * slots_sent, model_width // half_cou...  3.72 us
    pallas_call x1, Pallas kernels, per_device(): call(attend_kernel, [shape(rows // 2, model_width, kind=f32), shape(rows...  3.11 us
    pallas_call x2, Pallas kernels, per_device(): call(functools.partial(score_kernel, orders, halves, 1), shape(6 * len(or...  3.03 us
  transfers between devices with their start and end apart: 26, of which 17 were waited for; matrix products, arithmetic and copies ran while one was open for 0% of the time, Pallas kernels for 3%

profile of v1, /device:TPU:0, one launch (start us, length us, event | category | flops | bytes accessed | tf_op | source)
XLA Modules:
  0.0 108.1 jit_solution(11535593114304106021)
XLA Ops:
  3.4 3.0 %collective-permute-start.8 = (s32[24,8]{1,0:T(8,128)S(1)}, s32[24,8]{1,0:T(8,128)S(1)}, u32[]{:S(2)}, u32[]{:S(2)}) collective-permute-start(s32[24,8]{1,0:T(8,128)S(1)} %pad_add_fusion.2), channel_id=1, source_target_pairs={{0,8},{4,12},{8,0},{12,4},{16,24},{20,28},{24,16},{28,20},{1,9},{5... | collective-permute-start | bytes 2312 | tf_op jit(solution)/shard_map/ppermute | solution.py:528
  6.4 1.7 %collective-permute-done.8 = s32[24,8]{1,0:T(8,128)S(1)} collective-permute-done((s32[24,8]{1,0:T(8,128)S(1)}, s32[24,8]{1,0:T(8,128)S(1)}, u32[]{:S(2)}, u32[]{:S(2)}) %collective-permute-start.8) | collective-permute-done | bytes 800 | tf_op jit(solution)/shard_map/ppermute | solution.py:528
  8.1 3.1 %collective-permute-start.9 = (s32[48,8]{1,0:T(8,128)S(1)}, s32[48,8]{1,0:T(8,128)S(1)}, u32[]{:S(2)}, u32[]{:S(2)}) collective-permute-start(s32[48,8]{1,0:T(8,128)S(1)} %pad_add_fusion.1), channel_id=1, source_target_pairs={{0,16},{4,20},{8,24},{12,28},{16,0},{20,4},{24,8},{28,12},{1,17},{... | collective-permute-start | bytes 4616 | tf_op jit(solution)/shard_map/ppermute | solution.py:528
  11.2 1.8 %collective-permute-done.9 = s32[48,8]{1,0:T(8,128)S(1)} collective-permute-done((s32[48,8]{1,0:T(8,128)S(1)}, s32[48,8]{1,0:T(8,128)S(1)}, u32[]{:S(2)}, u32[]{:S(2)}) %collective-permute-start.9) | collective-permute-done | bytes 1568 | tf_op jit(solution)/shard_map/ppermute | solution.py:528
  13.0 3.7 %shard_map.185 = (bf16[24,2304]{1,0:T(8,128)(2,1)S(1)}, bf16[24,2304]{1,0:T(8,128)(2,1)S(1)}, bf16[24,2304]{1,0:T(8,128)(2,1)S(1)}, bf16[24,2304]{1,0:T(8,128)(2,1)S(1)}, s32[8,48]{1,0:T(8,128)S(1)}, /*index=5*/s32[1]{0:T(128)}) custom-call(s32[1]{0:T(128)} %copy.46.first_slot.slot, s32[96,8]{1,0:T(8,128)S(1)} %pad_add_fusion.ids.refs_0_, ...), custom_call_target="tpu_custom_call" | custom-call | flops 452984832 | bytes 4529848 | tf_op jit(solution)/shard_map/pallas_call | solution.py:555
  16.7 2.0 %collective-permute-start.10 = (bf16[24,2304]{1,0:T(8,128)(2,1)S(1)}, bf16[24,2304]{1,0:T(8,128)(2,1)S(1)}, u32[]{:S(2)}, u32[]{:S(2)}) collective-permute-start(bf16[24,2304]{1,0:T(8,128)(2,1)S(1)} %get-tuple-element.59), channel_id=1, source_target_pairs={{0,8},{4,12},{8,0},{12,4},{16,24},{20,28},{24,16},{28,20},{1,9},{5... | collective-permute-start | bytes 331784 | tf_op jit(solution)/shard_map/ppermute | solution.py:528
  18.7 2.7 %collective-permute-start.11 = (bf16[24,2304]{1,0:T(8,128)(2,1)S(1)}, bf16[24,2304]{1,0:T(8,128)(2,1)S(1)}, u32[]{:S(2)}, u32[]{:S(2)}) collective-permute-start(bf16[24,2304]{1,0:T(8,128)(2,1)S(1)} %get-tuple-element.60), channel_id=1, source_target_pairs={{0,16},{4,20},{8,24},{12,28},{16,0},{20,4},{24,8},{28,12},{1,17},{... | collective-permute-start | bytes 331784 | tf_op jit(solution)/shard_map/ppermute | solution.py:528
  22.2 6.0 %collective-permute-done.11.refs_3_ = bf16[24,2304]{1,0:T(8,128)(2,1)S(1)} collective-permute-done((bf16[24,2304]{1,0:T(8,128)(2,1)S(1)}, bf16[24,2304]{1,0:T(8,128)(2,1)S(1)}, u32[]{:S(2)}, u32[]{:S(2)}) %collective-permute-start.11) | collective-permute-done | bytes 110624 | tf_op jit(solution)/shard_map/ppermute | solution.py:528
  33.5 3.9 %collective-permute-done.18 = bf16[48,2304]{1,0:T(8,128)(2,1)S(1)} collective-permute-done((bf16[48,2304]{1,0:T(8,128)(2,1)S(1)}, bf16[48,2304]{1,0:T(8,128)(2,1)S(1)}, u32[]{:S(2)}, u32[]{:S(2)}) %collective-permute-start.18) | collective-permute-done | bytes 221216 | tf_op jit(solution)/shard_map/ppermute | solution.py:536
  37.5 1.6 %collective-permute-start.20 = (bf16[48,2304]{1,0:T(8,128)(2,1)S(1)}, bf16[48,2304]{1,0:T(8,128)(2,1)S(1)}, u32[]{:S(2)}, u32[]{:S(2)}) collective-permute-start(bf16[48,2304]{1,0:T(8,128)(2,1)S(1)} %add.20.kept_second), channel_id=1, source_target_pairs={{0,2},{1,3},{2,0},{3,1},{4,5},{5,4},{6,7},{7,6},{8,10},{9,11},{10,... | collective-permute-start | bytes 663560 | tf_op jit(solution)/shard_map/ppermute | solution.py:536
  40.0 1.6 %collective-permute-start.19 = (bf16[48,2304]{1,0:T(8,128)(2,1)S(1)}, bf16[48,2304]{1,0:T(8,128)(2,1)S(1)}, u32[]{:S(2)}, u32[]{:S(2)}) collective-permute-start(bf16[48,2304]{1,0:T(8,128)(2,1)S(1)} %add.19.kept_first), channel_id=1, source_target_pairs={{0,2},{1,3},{2,0},{3,1},{4,5},{5,4},{6,7},{7,6},{8,10},{9,11},{10,... | collective-permute-start | bytes 663560 | tf_op jit(solution)/shard_map/ppermute | solution.py:536
  43.5 2.5 %collective-permute-done.19.got_first = bf16[48,2304]{1,0:T(8,128)(2,1)S(1)} collective-permute-done((bf16[48,2304]{1,0:T(8,128)(2,1)S(1)}, bf16[48,2304]{1,0:T(8,128)(2,1)S(1)}, u32[]{:S(2)}, u32[]{:S(2)}) %collective-permute-start.19) | collective-permute-done | bytes 221216 | tf_op jit(solution)/shard_map/ppermute | solution.py:536
  46.0 3.1 %shard_map.188 = (f32[24,4608]{1,0:T(8,128)S(1)}, bf16[24,4608]{1,0:T(8,128)(2,1)S(1)}, bf16[12,4608]{1,0:T(8,128)(2,1)S(1)}) custom-call(s32[2,2]{1,0:T(2,128)S(1)} %copy-done.8, s32[2,2]{1,0:T(2,128)S(1)} %copy-done.9, s32[2]{0:T(128)S(1)} %copy-done.10, bf16[48,2304]{1,0:T(8,128)(2,1)S(1)} %add.19.kept_first, bf16[48,2304]{1,0:T(8,128)(2,1)S(1)} %add.20.kept_second, ...), custom_call_target="tpu_custom_call" | custom-call | flops 339738624 | bytes 3397386 | tf_op jit(solution)/shard_map/pallas_call | solution.py:614
  50.7 4.4 %collective-permute-done.21.got = bf16[24,4608]{1,0:T(8,128)(2,1)S(1)} collective-permute-done((bf16[24,4608]{1,0:T(8,128)(2,1)S(1)}, bf16[24,4608]{1,0:T(8,128)(2,1)S(1)}, u32[]{:S(2)}, u32[]{:S(2)}) %collective-permute-start.21) | collective-permute-done | bytes 221216 | tf_op jit(solution)/shard_map/ppermute | solution.py:536
  55.2 1.6 %collective-permute-start.22 = (bf16[12,4608]{1,0:T(8,128)(2,1)S(1)}, bf16[12,4608]{1,0:T(8,128)(2,1)S(1)}, u32[]{:S(2)}, u32[]{:S(2)}) collective-permute-start(bf16[12,4608]{1,0:T(8,128)(2,1)S(1)} %get-tuple-element.72), channel_id=1, source_target_pairs={{0,2},{1,3},{2,0},{3,1},{4,5},{5,4},{6,7},{7,6},{8,10},{9,11},{10,... | collective-permute-start | bytes 331784 | tf_op jit(solution)/shard_map/ppermute | solution.py:536
  56.9 3.6 %collective-permute-done.22.got = bf16[12,4608]{1,0:T(8,128)(2,1)S(1)} collective-permute-done((bf16[12,4608]{1,0:T(8,128)(2,1)S(1)}, bf16[12,4608]{1,0:T(8,128)(2,1)S(1)}, u32[]{:S(2)}, u32[]{:S(2)}) %collective-permute-start.22) | collective-permute-done | bytes 110624 | tf_op jit(solution)/shard_map/ppermute | solution.py:536
  60.8 2.5 %collective-permute-start.25 = (bf16[24,2304]{1,0:T(8,128)(2,1)S(1)}, bf16[24,2304]{1,0:T(8,128)(2,1)S(1)}, u32[]{:S(2)}, u32[]{:S(2)}) collective-permute-start(bf16[24,2304]{1,0:T(8,128)(2,1)S(1)} %shard_map.190.refs_0_), channel_id=1, source_target_pairs={{0,24},{4,28},{8,16},{12,20},{16,8},{20,12},{24,0},{28,4},{1,25},{... | collective-permute-start | bytes 331784 | tf_op jit(solution)/shard_map/ppermute | solution.py:528
  65.2 2.3 %collective-permute-done.25.refs_3_ = bf16[24,2304]{1,0:T(8,128)(2,1)S(1)} collective-permute-done((bf16[24,2304]{1,0:T(8,128)(2,1)S(1)}, bf16[24,2304]{1,0:T(8,128)(2,1)S(1)}, u32[]{:S(2)}, u32[]{:S(2)}) %collective-permute-start.25) | collective-permute-done | bytes 110624 | tf_op jit(solution)/shard_map/ppermute | solution.py:528
  67.5 2.9 %collective-permute-done.24.refs_2_ = bf16[24,2304]{1,0:T(8,128)(2,1)S(1)} collective-permute-done((bf16[24,2304]{1,0:T(8,128)(2,1)S(1)}, bf16[24,2304]{1,0:T(8,128)(2,1)S(1)}, u32[]{:S(2)}, u32[]{:S(2)}) %collective-permute-start.24) | collective-permute-done | bytes 110624 | tf_op jit(solution)/shard_map/ppermute | solution.py:528
  70.4 1.6 %collective-permute-start.26 = (bf16[48,4608]{1,0:T(8,128)(2,1)S(1)}, bf16[48,4608]{1,0:T(8,128)(2,1)S(1)}, u32[]{:S(2)}, u32[]{:S(2)}) collective-permute-start(bf16[48,4608]{1,0:T(8,128)(2,1)S(1)} %shard_map.191.refs_0_), channel_id=1, source_target_pairs={{0,2},{1,3},{2,0},{3,1},{4,5},{5,4},{6,7},{7,6},{8,10},{9,11},{10,... | collective-permute-start | bytes 1327112 | tf_op jit(solution)/shard_map/ppermute | solution.py:536
  73.5 8.9 %collective-permute-done.26.refs_0_ = bf16[48,4608]{1,0:T(8,128)(2,1)S(1)} collective-permute-done((bf16[48,4608]{1,0:T(8,128)(2,1)S(1)}, bf16[48,4608]{1,0:T(8,128)(2,1)S(1)}, u32[]{:S(2)}, u32[]{:S(2)}) %collective-permute-start.26) | collective-permute-done | bytes 442400 | tf_op jit(solution)/shard_map/ppermute | solution.py:536
  84.4 6.3 %collective-permute-done.27.refs_0_ = bf16[48,4608]{1,0:T(8,128)(2,1)S(1)} collective-permute-done((bf16[48,4608]{1,0:T(8,128)(2,1)S(1)}, bf16[48,4608]{1,0:T(8,128)(2,1)S(1)}, u32[]{:S(2)}, u32[]{:S(2)}) %collective-permute-start.27) | collective-permute-done | bytes 442400 | tf_op jit(solution)/shard_map/ppermute | solution.py:536
  92.1 1.6 %shard_map.193.refs_5_ = f32[12,48]{1,0:T(8,128)S(1)} custom-call(bf16[48,4608]{1,0:T(8,128)(2,1)S(1)} %collective-permute-done.26.refs_0_, bf16[48,4608]{1,0:T(8,128)(2,1)S(1)} %collective-permute-done.30.refs_1_, bf16[48,4608]{1,0:T(8,128)(2,1)S(1)} %collective-permute-done.31.refs_2_, bf16[48,4608]{1,0:T(8,128)(2,1)S(1)} %collective-permute-done.32.refs_3_, ...), custom_call_target="tpu_custom_call" | custom-call | flops 905969664 | bytes 9059696 | tf_op jit(solution)/shard_map/pallas_call | solution.py:680
  95.2 12.1 %all_to_all.11 = f32[32,4,128]{2,1,0:T(4,128)S(1)} all-to-all(f32[32,4,128]{2,1,0:T(4,128)S(1)} %bitcast.4), channel_id=1, replica_groups=mesh['batch'=8,'vocab'=4] {'batch','vocab'}, dimensions={0} | all-to-all | bytes 131072 | tf_op jit(solution)/shard_map/all_to_all | solution.py:696
  (84 shorter events, 22.8 us)
Async XLA Ops:
  3.4 4.6 %collective-permute-start.8 = (s32[24,8]{1,0:T(8,128)S(1)}, s32[24,8]{1,0:T(8,128)S(1)}, u32[]{:S(2)}, u32[]{:S(2)}) collective-permute-start(s32[24,8]{1,0:T(8,128)S(1)} %pad_add_fusion.2), channel_id=1, source_target_pairs={{0,8},{4,12},{8,0},{12,4},{16,24},{20,28},{24,16},{28,20},{1,9},{5... | collective-permute-start | bytes 2312 | tf_op jit(solution)/shard_map/ppermute | solution.py:528
  8.1 4.9 %collective-permute-start.9 = (s32[48,8]{1,0:T(8,128)S(1)}, s32[48,8]{1,0:T(8,128)S(1)}, u32[]{:S(2)}, u32[]{:S(2)}) collective-permute-start(s32[48,8]{1,0:T(8,128)S(1)} %pad_add_fusion.1), channel_id=1, source_target_pairs={{0,16},{4,20},{8,24},{12,28},{16,0},{20,4},{24,8},{28,12},{1,17},{... | collective-permute-start | bytes 4616 | tf_op jit(solution)/shard_map/ppermute | solution.py:528
  16.7 5.4 %collective-permute-start.10 = (bf16[24,2304]{1,0:T(8,128)(2,1)S(1)}, bf16[24,2304]{1,0:T(8,128)(2,1)S(1)}, u32[]{:S(2)}, u32[]{:S(2)}) collective-permute-start(bf16[24,2304]{1,0:T(8,128)(2,1)S(1)} %get-tuple-element.59), channel_id=1, source_target_pairs={{0,8},{4,12},{8,0},{12,4},{16,24},{20,28},{24,16},{28,20},{1,9},{5... | collective-permute-start | bytes 331784 | tf_op jit(solution)/shard_map/ppermute | solution.py:528
  18.7 9.4 %collective-permute-start.11 = (bf16[24,2304]{1,0:T(8,128)(2,1)S(1)}, bf16[24,2304]{1,0:T(8,128)(2,1)S(1)}, u32[]{:S(2)}, u32[]{:S(2)}) collective-permute-start(bf16[24,2304]{1,0:T(8,128)(2,1)S(1)} %get-tuple-element.60), channel_id=1, source_target_pairs={{0,16},{4,20},{8,24},{12,28},{16,0},{20,4},{24,8},{28,12},{1,17},{... | collective-permute-start | bytes 331784 | tf_op jit(solution)/shard_map/ppermute | solution.py:528
  21.4 6.7 %collective-permute-start.12 = (bf16[24,2304]{1,0:T(8,128)(2,1)S(1)}, bf16[24,2304]{1,0:T(8,128)(2,1)S(1)}, u32[]{:S(2)}, u32[]{:S(2)}) collective-permute-start(bf16[24,2304]{1,0:T(8,128)(2,1)S(1)} %get-tuple-element.61), channel_id=1, source_target_pairs={{0,24},{4,28},{8,16},{12,20},{16,8},{20,12},{24,0},{28,4},{1,25},{... | collective-permute-start | bytes 331784 | tf_op jit(solution)/shard_map/ppermute | solution.py:528
  21.4 7.2 %collective-permute-start.13 = (bf16[24,2304]{1,0:T(8,128)(2,1)S(1)}, bf16[24,2304]{1,0:T(8,128)(2,1)S(1)}, u32[]{:S(2)}, u32[]{:S(2)}) collective-permute-start(bf16[24,2304]{1,0:T(8,128)(2,1)S(1)} %get-tuple-element.58.refs_1_), channel_id=1, source_target_pairs={{0,4},{4,0},{8,12},{12,8},{16,20},{20,16},{24,28},{28,24},{1,5},{5... | collective-permute-start | bytes 331784 | tf_op jit(solution)/shard_map/ppermute | solution.py:528
  22.2 6.5 %collective-permute-start.14 = (bf16[24,2304]{1,0:T(8,128)(2,1)S(1)}, bf16[24,2304]{1,0:T(8,128)(2,1)S(1)}, u32[]{:S(2)}, u32[]{:S(2)}) collective-permute-start(bf16[24,2304]{1,0:T(8,128)(2,1)S(1)} %collective-permute-done.10.refs_2_), channel_id=1, source_target_pairs={{0,4},{4,0},{8,12},{12,8},{16,20},{20,16},{24,28},{28,24},{1,5},{5... | collective-permute-start | bytes 331784 | tf_op jit(solution)/shard_map/ppermute | solution.py:528
  28.1 1.5 %collective-permute-start.16 = (bf16[24,2304]{1,0:T(8,128)(2,1)S(1)}, bf16[24,2304]{1,0:T(8,128)(2,1)S(1)}, u32[]{:S(2)}, u32[]{:S(2)}) collective-permute-start(bf16[24,2304]{1,0:T(8,128)(2,1)S(1)} %collective-permute-done.12.refs_4_), channel_id=1, source_target_pairs={{0,4},{4,0},{8,12},{12,8},{16,20},{20,16},{24,28},{28,24},{1,5},{5... | collective-permute-start | bytes 331784 | tf_op jit(solution)/shard_map/ppermute | solution.py:528
  31.4 6.0 %collective-permute-start.18 = (bf16[48,2304]{1,0:T(8,128)(2,1)S(1)}, bf16[48,2304]{1,0:T(8,128)(2,1)S(1)}, u32[]{:S(2)}, u32[]{:S(2)}) collective-permute-start(bf16[48,2304]{1,0:T(8,128)(2,1)S(1)} %get-tuple-element.66), channel_id=1, source_target_pairs={{0,1},{1,0},{2,3},{3,2},{4,6},{5,7},{6,4},{7,5},{8,9},{9,8},{10,11... | collective-permute-start | bytes 663560 | tf_op jit(solution)/shard_map/ppermute | solution.py:536
  33.0 6.9 %collective-permute-start.17 = (bf16[48,2304]{1,0:T(8,128)(2,1)S(1)}, bf16[48,2304]{1,0:T(8,128)(2,1)S(1)}, u32[]{:S(2)}, u32[]{:S(2)}) collective-permute-start(bf16[48,2304]{1,0:T(8,128)(2,1)S(1)} %get-tuple-element.65), channel_id=1, source_target_pairs={{0,1},{1,0},{2,3},{3,2},{4,6},{5,7},{6,4},{7,5},{8,9},{9,8},{10,11... | collective-permute-start | bytes 663560 | tf_op jit(solution)/shard_map/ppermute | solution.py:536
  37.5 6.0 %collective-permute-start.20 = (bf16[48,2304]{1,0:T(8,128)(2,1)S(1)}, bf16[48,2304]{1,0:T(8,128)(2,1)S(1)}, u32[]{:S(2)}, u32[]{:S(2)}) collective-permute-start(bf16[48,2304]{1,0:T(8,128)(2,1)S(1)} %add.20.kept_second), channel_id=1, source_target_pairs={{0,2},{1,3},{2,0},{3,1},{4,5},{5,4},{6,7},{7,6},{8,10},{9,11},{10,... | collective-permute-start | bytes 663560 | tf_op jit(solution)/shard_map/ppermute | solution.py:536
  40.0 6.0 %collective-permute-start.19 = (bf16[48,2304]{1,0:T(8,128)(2,1)S(1)}, bf16[48,2304]{1,0:T(8,128)(2,1)S(1)}, u32[]{:S(2)}, u32[]{:S(2)}) collective-permute-start(bf16[48,2304]{1,0:T(8,128)(2,1)S(1)} %add.19.kept_first), channel_id=1, source_target_pairs={{0,2},{1,3},{2,0},{3,1},{4,5},{5,4},{6,7},{7,6},{8,10},{9,11},{10,... | collective-permute-start | bytes 663560 | tf_op jit(solution)/shard_map/ppermute | solution.py:536
  49.2 6.0 %collective-permute-start.21 = (bf16[24,4608]{1,0:T(8,128)(2,1)S(1)}, bf16[24,4608]{1,0:T(8,128)(2,1)S(1)}, u32[]{:S(2)}, u32[]{:S(2)}) collective-permute-start(bf16[24,4608]{1,0:T(8,128)(2,1)S(1)} %get-tuple-element.70), channel_id=1, source_target_pairs={{0,1},{1,0},{2,3},{3,2},{4,6},{5,7},{6,4},{7,5},{8,9},{9,8},{10,11... | collective-permute-start | bytes 663560 | tf_op jit(solution)/shard_map/ppermute | solution.py:536
  55.2 5.2 %collective-permute-start.22 = (bf16[12,4608]{1,0:T(8,128)(2,1)S(1)}, bf16[12,4608]{1,0:T(8,128)(2,1)S(1)}, u32[]{:S(2)}, u32[]{:S(2)}) collective-permute-start(bf16[12,4608]{1,0:T(8,128)(2,1)S(1)} %get-tuple-element.72), channel_id=1, source_target_pairs={{0,2},{1,3},{2,0},{3,1},{4,5},{5,4},{6,7},{7,6},{8,10},{9,11},{10,... | collective-permute-start | bytes 331784 | tf_op jit(solution)/shard_map/ppermute | solution.py:536
  60.8 6.7 %collective-permute-start.25 = (bf16[24,2304]{1,0:T(8,128)(2,1)S(1)}, bf16[24,2304]{1,0:T(8,128)(2,1)S(1)}, u32[]{:S(2)}, u32[]{:S(2)}) collective-permute-start(bf16[24,2304]{1,0:T(8,128)(2,1)S(1)} %shard_map.190.refs_0_), channel_id=1, source_target_pairs={{0,24},{4,28},{8,16},{12,20},{16,8},{20,12},{24,0},{28,4},{1,25},{... | collective-permute-start | bytes 331784 | tf_op jit(solution)/shard_map/ppermute | solution.py:528
  63.3 7.1 %collective-permute-start.24 = (bf16[24,2304]{1,0:T(8,128)(2,1)S(1)}, bf16[24,2304]{1,0:T(8,128)(2,1)S(1)}, u32[]{:S(2)}, u32[]{:S(2)}) collective-permute-start(bf16[24,2304]{1,0:T(8,128)(2,1)S(1)} %shard_map.190.refs_0_), channel_id=1, source_target_pairs={{0,16},{4,20},{8,24},{12,28},{16,0},{20,4},{24,8},{28,12},{1,17},{... | collective-permute-start | bytes 331784 | tf_op jit(solution)/shard_map/ppermute | solution.py:528
  64.1 6.3 %collective-permute-start.23 = (bf16[24,2304]{1,0:T(8,128)(2,1)S(1)}, bf16[24,2304]{1,0:T(8,128)(2,1)S(1)}, u32[]{:S(2)}, u32[]{:S(2)}) collective-permute-start(bf16[24,2304]{1,0:T(8,128)(2,1)S(1)} %shard_map.190.refs_0_), channel_id=1, source_target_pairs={{0,8},{4,12},{8,0},{12,4},{16,24},{20,28},{24,16},{28,20},{1,9},{5... | collective-permute-start | bytes 331784 | tf_op jit(solution)/shard_map/ppermute | solution.py:528
  70.4 11.9 %collective-permute-start.26 = (bf16[48,4608]{1,0:T(8,128)(2,1)S(1)}, bf16[48,4608]{1,0:T(8,128)(2,1)S(1)}, u32[]{:S(2)}, u32[]{:S(2)}) collective-permute-start(bf16[48,4608]{1,0:T(8,128)(2,1)S(1)} %shard_map.191.refs_0_), channel_id=1, source_target_pairs={{0,2},{1,3},{2,0},{3,1},{4,5},{5,4},{6,7},{7,6},{8,10},{9,11},{10,... | collective-permute-start | bytes 1327112 | tf_op jit(solution)/shard_map/ppermute | solution.py:536
  72.0 11.8 %collective-permute-start.30 = (bf16[48,4608]{1,0:T(8,128)(2,1)S(1)}, bf16[48,4608]{1,0:T(8,128)(2,1)S(1)}, u32[]{:S(2)}, u32[]{:S(2)}) collective-permute-start(bf16[48,4608]{1,0:T(8,128)(2,1)S(1)} %shard_map.191.refs_0_), channel_id=1, source_target_pairs={{0,1},{1,0},{2,3},{3,2},{4,6},{5,7},{6,4},{7,5},{8,9},{9,8},{10,11... | collective-permute-start | bytes 1327112 | tf_op jit(solution)/shard_map/ppermute | solution.py:536
  82.4 8.3 %collective-permute-start.27 = (bf16[48,4608]{1,0:T(8,128)(2,1)S(1)}, bf16[48,4608]{1,0:T(8,128)(2,1)S(1)}, u32[]{:S(2)}, u32[]{:S(2)}) collective-permute-start(bf16[48,4608]{1,0:T(8,128)(2,1)S(1)} %collective-permute-done.26.refs_0_), channel_id=1, source_target_pairs={{0,1},{1,0},{2,3},{3,2},{4,6},{5,7},{6,4},{7,5},{8,9},{9,8},{10,11... | collective-permute-start | bytes 1327112 | tf_op jit(solution)/shard_map/ppermute | solution.py:536
  83.9 6.8 %collective-permute-start.29 = (bf16[48,4608]{1,0:T(8,128)(2,1)S(1)}, bf16[48,4608]{1,0:T(8,128)(2,1)S(1)}, u32[]{:S(2)}, u32[]{:S(2)}) collective-permute-start(bf16[48,4608]{1,0:T(8,128)(2,1)S(1)} %shard_map.191.refs_0_), channel_id=1, source_target_pairs={{0,4},{4,0},{8,12},{12,8},{16,20},{20,16},{24,28},{28,24},{1,5},{5... | collective-permute-start | bytes 1327112 | tf_op jit(solution)/shard_map/ppermute | solution.py:528
  83.9 8.3 %collective-permute-start.32 = (bf16[48,4608]{1,0:T(8,128)(2,1)S(1)}, bf16[48,4608]{1,0:T(8,128)(2,1)S(1)}, u32[]{:S(2)}, u32[]{:S(2)}) collective-permute-start(bf16[48,4608]{1,0:T(8,128)(2,1)S(1)} %collective-permute-done.30.refs_1_), channel_id=1, source_target_pairs={{0,4},{4,0},{8,12},{12,8},{16,20},{20,16},{24,28},{28,24},{1,5},{5... | collective-permute-start | bytes 1327112 | tf_op jit(solution)/shard_map/ppermute | solution.py:528
  84.4 7.8 %collective-permute-start.31 = (bf16[48,4608]{1,0:T(8,128)(2,1)S(1)}, bf16[48,4608]{1,0:T(8,128)(2,1)S(1)}, u32[]{:S(2)}, u32[]{:S(2)}) collective-permute-start(bf16[48,4608]{1,0:T(8,128)(2,1)S(1)} %collective-permute-done.26.refs_0_), channel_id=1, source_target_pairs={{0,4},{4,0},{8,12},{12,8},{16,20},{20,16},{24,28},{28,24},{1,5},{5... | collective-permute-start | bytes 1327112 | tf_op jit(solution)/shard_map/ppermute | solution.py:528
  90.7 3.0 %collective-permute-start.28 = (bf16[48,4608]{1,0:T(8,128)(2,1)S(1)}, bf16[48,4608]{1,0:T(8,128)(2,1)S(1)}, u32[]{:S(2)}, u32[]{:S(2)}) collective-permute-start(bf16[48,4608]{1,0:T(8,128)(2,1)S(1)} %collective-permute-done.27.refs_0_), channel_id=1, source_target_pairs={{0,4},{4,0},{8,12},{12,8},{16,20},{20,16},{24,28},{28,24},{1,5},{5... | collective-permute-start | bytes 1327112 | tf_op jit(solution)/shard_map/ppermute | solution.py:528
  (19 other events, 202.5 us)

commit v2 on v1

--- a/solution.py
+++ b/solution.py
@@ -92,12 +92,19 @@
             ids[first : first + windows.shape[1], :] = held[kind, at]
 
 
-def send_kernel(first_slot, ids, table, *outs):
+def load_kernel(start, source, target, done):
+    copy = pltpu.make_async_copy(source.at[pl.ds(start, target.shape[0])], target, done)
+    copy.start()
+    copy.wait()
+
+
+def send_kernel(first_slot, ids, upper, lower, *outs):
     batch_devices = lax.axis_size("batch")
     vocab_devices = lax.axis_size("vocab")
     far = batch_devices // 2
     at_core = lax.axis_index("batch") % 2
-    vocab_rows, model_width = table.shape
+    part_rows, model_width = upper.shape
+    vocab_rows = 2 * part_rows
     first = (lax.axis_index("batch") * vocab_devices + lax.axis_index("vocab")) * vocab_rows
     sent, pools, most = outs[:far], outs[far], outs[far + 1]
     stride = ids.shape[0] // batch_devices
@@ -118,11 +125,13 @@
     wide = model_width // half_count
     rows = jnp.zeros((one_hot.shape[0], wide), f32)
     for half in range(half_count):
-        rows = rows + jnp.dot(
-            jnp.where(half_of == half, one_hot, 0.0).astype(bf16),
-            table[:, half * wide : (half + 1) * wide],
-            preferred_element_type=f32,
-        )
+        chosen = jnp.where(half_of == half, one_hot, 0.0).astype(bf16)
+        for at, part in enumerate((upper, lower)):
+            rows = rows + jnp.dot(
+                chosen[:, at * part_rows : (at + 1) * part_rows],
+                part[:, half * wide : (half + 1) * wide],
+                preferred_element_type=f32,
+            )
     for at in range(far):
         sent[at][...] = rows[at * block : (at + 1) * block].astype(bf16)
     owner = lax.div(tokens, jnp.full_like(tokens, vocab_rows)).astype(f32)
@@ -183,6 +192,13 @@
     sine[...] = jnp.sin(angles) * signs[...]
 
 
+def stacked(values):
+    wide = values.shape[1] // half_count
+    return jnp.concatenate(
+        [values[:, half * wide : (half + 1) * wide] for half in range(half_count)], axis=0
+    )
+
+
 def attend_kernel(
     accepted,
     converged,
@@ -201,8 +217,8 @@
     cache_keys,
     cache_values,
     keep,
-    send,
     own,
+    *sends,
 ):
     rows = got_first.shape[0]
     model_width = w_query.shape[0]
@@ -212,7 +228,6 @@
     tokens = iter_count * width
     chunk = own.shape[0]
     at_vocab = lax.axis_index("vocab")
-    at_core = lax.axis_index("batch") % 2
     gathered = jnp.concatenate(
         [
             kept_first[...].astype(f32) + got_first[...].astype(f32),
@@ -293,7 +308,7 @@
     attended = jnp.concatenate(attended_rows, axis=0).astype(bf16)
 
     ordered = iota((rows, rows), 0)
-    wanted = owner_of(ordered // chunk, at_vocab, at_core) * chunk + ordered % chunk
+    wanted = ((ordered // chunk) ^ at_vocab) * chunk + ordered % chunk
     place = iota((rows, rows), 1)
     at_batch = place // tokens
     at_window = (place % tokens) // width
@@ -302,39 +317,41 @@
     by_window = jnp.where(wanted == place, 1.0, 0.0)[:chunk].astype(bf16)
     own[...] = jnp.dot(by_window, gathered.astype(bf16), preferred_element_type=f32).astype(bf16)
     attended = jnp.dot(by_sequence, attended, preferred_element_type=f32).astype(bf16)
-    half = rows // 2
-    send[...] = jnp.dot(attended[half:], w_out[...], preferred_element_type=f32).astype(bf16)
-    keep[...] = jnp.dot(attended[:half], w_out[...], preferred_element_type=f32)
-
-
-def halve_kernel(kept, got, keep, send):
-    half = keep.shape[0]
-    total = kept[...] + got[...].astype(f32)
-    keep[...] = total[:half]
-    send[...] = total[half:].astype(bf16)
-
-
-def final_kernel(kept, got, own, post_gain, final_gain, final):
-    model_width = kept.shape[1]
-    branch = kept[...] + got[...].astype(f32)
+    branch = jnp.dot(attended, w_out[...], preferred_element_type=f32)
+    keep[...] = branch[:chunk]
+    for at, ref in enumerate(sends):
+        ref[...] = stacked(branch[(at + 1) * chunk : (at + 2) * chunk]).astype(bf16)
+
+
+def final_kernel(kept, own, post_gain, final_gain, *refs):
+    parts, final = refs[:-1], refs[-1]
+    chunk, model_width = kept.shape
+    total = jnp.zeros((half_count * chunk, model_width // half_count), f32)
+    for part in parts:
+        total = total + part[...].astype(f32)
+    branch = kept[...] + jnp.concatenate(
+        [total[half * chunk : (half + 1) * chunk] for half in range(half_count)], axis=1
+    )
     embedded = own[...].astype(f32) * math.sqrt(model_width)
     hidden = embedded + normalize(branch, post_gain[...])
-    rows = normalize(hidden, final_gain[...])
-    wide = model_width // half_count
-    final[...] = jnp.concatenate(
-        [rows[:, half * wide : (half + 1) * wide] for half in range(half_count)], axis=0
-    ).astype(bf16)
-
-
-def assemble_kernel(*refs):
-    parts, block = refs[:-1], refs[-1]
-    wide = parts[0].shape[1]
-    chunk = parts[0].shape[0] // half_count
-    values = [part[...].astype(f32) for part in parts]
-    for half in range(half_count):
-        block[:, half * wide : (half + 1) * wide] = jnp.concatenate(
-            [value[half * chunk : (half + 1) * chunk] for value in values], axis=0
-        ).astype(bf16)
+    final[...] = stacked(normalize(hidden, final_gain[...])).astype(bf16)
+
+
+def join_kernel(*refs):
+    parts, joint = refs[:-1], refs[-1]
+    joint[...] = jnp.concatenate([part[...].astype(f32) for part in parts], axis=0).astype(bf16)
+
+
+def half_of_block(near, distant, half):
+    size = near.shape[0]
+    chunk = size // half_count
+    count = distant.shape[0] // size
+    parts = [near[...].astype(f32)[half * chunk : (half + 1) * chunk]]
+    values = distant[...].astype(f32)
+    for at in range(count):
+        start = at * size + half * chunk
+        parts.append(values[start : start + chunk])
+    return jnp.concatenate(parts, axis=0)
 
 
 def score_blocks(blocks, core_of, order_of, tables, pools):
@@ -343,8 +360,8 @@
     at_vocab = lax.axis_index("vocab")
     at_core = lax.axis_index("batch") % 2
     far = lax.axis_size("batch") // 2
-    block_rows = blocks[0][0].shape[0]
-    chunk = block_rows // far
+    chunk = blocks[0][0].shape[0] // half_count
+    block_rows = chunk * far
     first = (lax.axis_index("batch") * vocab_devices + at_vocab) * vocab_rows
     wanted = []
     for other, order in zip(core_of, order_of):
@@ -361,8 +378,8 @@
         wanted.append(jnp.concatenate(parts, axis=1))
     wanted = jnp.concatenate(wanted, axis=1) - first
     values = [
-        jnp.concatenate([block[half][...] for block in blocks], axis=0)
-        for half in range(len(blocks[0]))
+        jnp.concatenate([half_of_block(*block, half) for block in blocks], axis=0).astype(bf16)
+        for half in range(half_count)
     ]
     wide = values[0].shape[1]
     sums, chosen, largest = [], [], []
@@ -395,27 +412,27 @@
 def score_kernel(orders, halves, parts, *refs):
     pools, scores = refs[-2:]
     tables = refs[len(refs) - 2 - parts : -2]
-    blocks = [refs[at * halves : (at + 1) * halves] for at in range(2 * len(orders))]
-    found = score_blocks(blocks, [0] * len(orders) + [1] * len(orders), orders * 2, tables, pools)
+    count = (len(refs) - parts - 2) // halves
+    blocks = [refs[at * halves : (at + 1) * halves] for at in range(count)]
+    cores = [0, 1] if len(blocks) > len(orders) else [0]
+    core_of = [core for core in cores for _ in orders]
+    found = score_blocks(blocks, core_of, orders * len(cores), tables, pools)
     for kind in range(3):
         for at in range(len(blocks)):
             row = kind * len(blocks) + at
             scores[row : row + 1, :] = found[kind][at]
 
 
-def late_kernel(orders, halves, parts, *refs):
+def late_kernel(orders, *refs):
     vocab_devices = lax.axis_size("vocab")
     at_vocab = lax.axis_index("vocab")
     at_batch = lax.axis_index("batch")
     far = lax.axis_size("batch") // 2
     message = refs[-1]
-    scores = refs[-1 - len(orders) : -1]
-    pools = refs[-2 - len(orders)]
-    tables = refs[2 * halves : 2 * halves + parts]
-    blocks = [refs[:halves], refs[halves : 2 * halves]]
-    block_rows = blocks[0][0].shape[0]
-    chunk = block_rows // far
-    late = score_blocks(blocks, [0, 1], [vocab_devices - 1] * 2, tables, pools)
+    scores = refs[-2 - len(orders) : -1]
+    block, tables, pools = refs[:2], refs[2:4], refs[4]
+    chunk = block[0].shape[0] // half_count
+    late = score_blocks([block], [1], [vocab_devices - 1], tables, pools)
     for other in range(2):
         kinds = []
         for kind in range(3):
@@ -423,7 +440,7 @@
             for group, score in zip(orders, scores):
                 row = (kind * 2 + other) * len(group)
                 found += [score[row + at : row + at + 1, :] for at in range(len(group))]
-            found.append(late[kind][other])
+            found.append(scores[-1][kind : kind + 1, :] if other == 0 else late[kind][0])
             owners = [
                 owner_of(jnp.int32(at), at_vocab, (at_batch % 2) ^ other)
                 for at in range(vocab_devices)
@@ -545,22 +562,37 @@
             pltpu.VMEM((2, iter_count, local_batch, width), jnp.int32),
             pltpu.SemaphoreType.DMA((2,)),
         ],
-        grant=2,
+        grant=60,
     )(window_ids, pool_ids)
     all_ids = own_ids
     for bit in bits_of(batch_devices):
         all_ids = jnp.concatenate([all_ids, batch_swap(all_ids, bit)], axis=0)
+
+    part_rows = vocab_rows // 2
+    tables = []
+    for at in range(2):
+        tables.append(
+            call(
+                functools.partial(load_kernel, at * part_rows),
+                shape(part_rows, model_width),
+                [pl.BlockSpec(memory_space=pl.ANY)],
+                vmem,
+                flops=10**8,
+                scratch=[pltpu.SemaphoreType.DMA(())],
+                grant=57,
+            )(table)
+        )
 
     def exchange(first_slot):
         *sent, pools, most = call(
             send_kernel,
             [shape(half_count * slots_sent, model_width // half_count)] * far
             + [shape(batch_devices, rows, kind=jnp.int32), shape(1, kind=jnp.int32)],
-            [smem, vmem, vmem],
+            [smem, vmem, vmem, vmem],
             [vmem] * (far + 1) + [smem],
             flops=2 * batch_devices * slots_sent * vocab_rows * model_width,
             grant=10,
-        )(first_slot, all_ids, table)
+        )(first_slot, all_ids, *tables)
         got = [sent[0]]
         for mask in range(1, far):
             got.append(batch_swap(sent[mask], 2 * mask))
@@ -611,15 +643,15 @@
     )
 
     wide = w_query.shape[1] + w_key.shape[1] + w_value.shape[1]
-    keep, send, own = call(
+    keep, own, *sends = call(
         attend_kernel,
         [
-            shape(rows // 2, model_width, kind=f32),
-            shape(rows // 2, model_width),
+            shape(chunk, model_width, kind=f32),
             shape(chunk, model_width),
-        ],
+        ]
+        + [shape(half_count * chunk, model_width // half_count)] * (vocab_devices - 1),
         [smem] * 3 + [vmem] * 13,
-        [vmem] * 3,
+        [vmem] * (vocab_devices + 1),
         flops=2 * rows * model_width * (wide + w_out.shape[0]),
         grant=20,
     )(
@@ -638,34 +670,39 @@
         cache_keys,
         cache_values,
     )
-    for step in range(len(vocab_bits) - 1):
-        half = keep.shape[0] // 2
-        keep, send = call(
-            halve_kernel,
-            [shape(half, model_width, kind=f32), shape(half, model_width)],
-            [vmem] * 2,
-            [vmem] * 2,
-        )(keep, mixed_swap(send, step))
+    branches = []
+    for at, send in enumerate(sends):
+        pairs = [(place, place ^ (at + 1)) for place in range(vocab_devices)]
+        branches.append(lax.ppermute(send, "vocab", pairs))
     final = call(
         final_kernel,
         shape(half_count * chunk, model_width // half_count),
-        [vmem] * 5,
+        [vmem] * (len(branches) + 4),
         vmem,
-    )(keep, mixed_swap(send, len(vocab_bits) - 1), own, post_gain[None], final_gain[None])
-
-    parts = [final]
+    )(keep, own, post_gain[None], final_gain[None], *branches)
+
+    parts = []
     for mask in range(1, far):
         parts.append(batch_swap(final, 2 * mask))
-    blocks = [
-        call(assemble_kernel, shape(far * chunk, model_width), [vmem] * far, vmem)(*parts)
-    ]
-    for step in range(len(vocab_bits)):
-        step = len(vocab_bits) - 1 - step
-        for at in range(len(blocks)):
-            blocks.append(mixed_swap(blocks[at], step))
-    halves = 1
-    own_blocks = [blocks]
-    other_blocks = [[batch_swap(each, 1) for each in blocks]]
+    joint = call(
+        join_kernel,
+        shape((far - 1) * half_count * chunk, model_width // half_count),
+        [vmem] * (far - 1),
+        vmem,
+    )(*parts)
+    halves = 2
+    own_blocks, other_blocks = [], []
+    for block in (final, joint):
+        blocks = [block]
+        for step in range(len(vocab_bits)):
+            step = len(vocab_bits) - 1 - step
+            for at in range(len(blocks)):
+                blocks.append(mixed_swap(blocks[at], step))
+        own_blocks.append(blocks)
+        others = []
+        for each in blocks:
+            others.append(batch_swap(each, 1))
+        other_blocks.append(others)
 
     per_block = 2 * far * chunk * vocab_rows * model_width
 
@@ -678,21 +715,31 @@
         inputs = halves_of(own_blocks, orders) + halves_of(other_blocks, orders)
         scores.append(
             call(
-                functools.partial(score_kernel, orders, halves, 1),
+                functools.partial(score_kernel, orders, halves, 2),
                 shape(6 * len(orders), far * chunk, kind=f32),
-                [vmem] * (len(inputs) + 1 + 1),
+                [vmem] * (len(inputs) + 3),
                 vmem,
                 flops=2 * per_block * len(orders),
-            )(*inputs, table, pools)
+                grant=6 + (16 * len(orders) * far * chunk * model_width >> 20),
+            )(*inputs, *tables, pools)
         )
-    last = [vocab_devices - 1]
+    last = vocab_devices - 1
+    scores.append(
+        call(
+            functools.partial(score_kernel, [last], halves, 2),
+            shape(3, far * chunk, kind=f32),
+            [vmem] * (halves + 3),
+            vmem,
+            flops=per_block,
+        )(*halves_of(own_blocks, [last]), *tables, pools)
+    )
     message = call(
-        functools.partial(late_kernel, groups_of, halves, 1),
+        functools.partial(late_kernel, groups_of),
         shape(all_devices * vocab_devices, lane_count, kind=f32),
-        [vmem] * (2 * halves + 1 + 1 + len(scores)),
+        [vmem] * (halves + 3 + len(scores)),
         vmem,
-        flops=2 * per_block,
-    )(*halves_of(own_blocks, last), *halves_of(other_blocks, last), table, pools, *scores)
+        flops=per_block,
+    )(*halves_of(other_blocks, [last]), *tables, pools, *scores)
     totals = lax.all_to_all(message, ("batch", "vocab"), 0, 0, tiled=True)
     return tuple(
         call(

time: 108 us -> 112 us (1.037)
  Pallas kernels: 14.1 us -> 17.5 us
  local copies, waits for them, and re-layouts: 1.5 us -> 0.14 us
    ppermute x0 -> x3, waiting for transfers between devices: none -> 5.11 us  [per_device(): branches.append(lax.ppermute(send, 'vocab', pairs))]
    pallas_call x6 -> x8, Pallas kernels: 7.78 us -> 12.2 us  [the longest x2 3.35 us: per_device(): call(functools.partial(load_kernel, at * part_rows), shape(part_rows, mod...]
    ppermute x9 -> x10, waiting for transfers between devices: 31.5 us -> 27.5 us  [mixed_swap(): return lax.ppermute(value, ('batch', 'vocab'), pairs)]
    ppermute x9 -> x10, starting transfers between devices: 13 us -> 9.39 us  [mixed_swap(): return lax.ppermute(value, ('batch', 'vocab'), pairs)]
    ppermute x0 -> x3, starting transfers between devices: none -> 3.55 us  [per_device(): branches.append(lax.ppermute(send, 'vocab', pairs))]
    pallas_call x1, Pallas kernels: 3.72 us -> 1.39 us  [exchange(): call(send_kernel, [shape(half_count * slots_sent, model_width // half_cou...]
    unnamed x34 -> x30, local copies, waits for them, and re-layouts: 1.46 us -> 0.09 us
    pallas_call x1, Pallas kernels: 0.03 us -> 1.31 us  [per_device(): call(pack_kernel, shape(2 * groups, width, kind=jnp.int32), [in_hbm] * 2,...]
  transfers between devices with their start and end apart: 26 -> 34, of which waited for: 17 -> 19; matrix products, arithmetic and copies ran while one was open for 0% -> 0% of each run, Pallas kernels for 3% -> 8%
where the time goes in v2:
time: 112 us
  waiting for transfers between devices  49.2 us (44%)
  starting transfers between devices  30.8 us (28%)
  Pallas kernels  17.5 us (16%)
  blocking collectives  11.3 us (10%)
    ppermute x10, waiting for transfers between devices, mixed_swap(): return lax.ppermute(value, ('batch', 'vocab'), pairs)  27.5 us
    ppermute x21, starting transfers between devices, batch_swap(): lax.ppermute(value, 'batch', [(at, at ^ mask) for at in range(batch_devic...  17.9 us
    ppermute x21, waiting for transfers between devices, batch_swap(): lax.ppermute(value, 'batch', [(at, at ^ mask) for at in range(batch_devic...  16.6 us
    all_to_all x1, blocking collectives, per_device(): totals = lax.all_to_all(message, ('batch', 'vocab'), 0, 0, tiled=True)  11.3 us
    ppermute x10, starting transfers between devices, mixed_swap(): return lax.ppermute(value, ('batch', 'vocab'), pairs)  9.39 us
    ppermute x3, waiting for transfers between devices, per_device(): branches.append(lax.ppermute(send, 'vocab', pairs))  5.11 us
    ppermute x3, starting transfers between devices, per_device(): branches.append(lax.ppermute(send, 'vocab', pairs))  3.55 us
    pallas_call x2, Pallas kernels, per_device(): call(functools.partial(load_kernel, at * part_rows), shape(part_rows, mod...  3.35 us
  transfers between devices with their start and end apart: 34, of which 19 were waited for; matrix products, arithmetic and copies ran while one was open for 0% of the time, Pallas kernels for 8%

profile of v2, /device:TPU:0, one launch (start us, length us, event | category | flops | bytes accessed | tf_op | source)
XLA Modules:
  0.0 111.8 jit_solution(13279375694191537841)
XLA Ops:
  4.3 3.0 %collective-permute-start.8 = (s32[24,8]{1,0:T(8,128)S(1)}, s32[24,8]{1,0:T(8,128)S(1)}, u32[]{:S(2)}, u32[]{:S(2)}) collective-permute-start(s32[24,8]{1,0:T(8,128)S(1)} %pad_add_fusion.2), channel_id=1, source_target_pairs={{0,8},{4,12},{8,0},{12,4},{16,24},{20,28},{24,16},{28,20},{1,9},{5... | collective-permute-start | bytes 2312 | tf_op jit(solution)/shard_map/ppermute | solution.py:545
  7.2 1.7 %shard_map.186.lower.refs_5_.refs_9_.refs_3_ = bf16[256,4608]{1,0:T(8,128)(2,1)S(1)} custom-call(bf16[512,4608]{1,0:T(8,128)(2,1)} %source.3), custom_call_target="tpu_custom_call" | custom-call | flops 100000000 | bytes 1000000 | tf_op jit(solution)/shard_map/pallas_call | solution.py:575
  8.9 3.1 %collective-permute-start.9 = (s32[48,8]{1,0:T(8,128)S(1)}, s32[48,8]{1,0:T(8,128)S(1)}, u32[]{:S(2)}, u32[]{:S(2)}) collective-permute-start(s32[48,8]{1,0:T(8,128)S(1)} %pad_add_fusion.1), channel_id=1, source_target_pairs={{0,16},{4,20},{8,24},{12,28},{16,0},{20,4},{24,8},{28,12},{1,17},{... | collective-permute-start | bytes 4616 | tf_op jit(solution)/shard_map/ppermute | solution.py:545
  12.0 1.7 %shard_map.185.upper.refs_4_.refs_8_.refs_2_ = bf16[256,4608]{1,0:T(8,128)(2,1)S(1)} custom-call(bf16[512,4608]{1,0:T(8,128)(2,1)} %source.3), custom_call_target="tpu_custom_call" | custom-call | flops 100000000 | bytes 1000000 | tf_op jit(solution)/shard_map/pallas_call | solution.py:575
  15.2 2.0 %collective-permute-start.10 = (bf16[24,2304]{1,0:T(8,128)(2,1)S(1)}, bf16[24,2304]{1,0:T(8,128)(2,1)S(1)}, u32[]{:S(2)}, u32[]{:S(2)}) collective-permute-start(bf16[24,2304]{1,0:T(8,128)(2,1)S(1)} %get-tuple-element.64), channel_id=1, source_target_pairs={{0,8},{4,12},{8,0},{12,4},{16,24},{20,28},{24,16},{28,20},{1,9},{5... | collective-permute-start | bytes 331784 | tf_op jit(solution)/shard_map/ppermute | solution.py:545
  17.2 2.7 %collective-permute-start.11 = (bf16[24,2304]{1,0:T(8,128)(2,1)S(1)}, bf16[24,2304]{1,0:T(8,128)(2,1)S(1)}, u32[]{:S(2)}, u32[]{:S(2)}) collective-permute-start(bf16[24,2304]{1,0:T(8,128)(2,1)S(1)} %get-tuple-element.65), channel_id=1, source_target_pairs={{0,16},{4,20},{8,24},{12,28},{16,0},{20,4},{24,8},{28,12},{1,17},{... | collective-permute-start | bytes 331784 | tf_op jit(solution)/shard_map/ppermute | solution.py:545
  21.0 6.0 %collective-permute-done.11.refs_3_ = bf16[24,2304]{1,0:T(8,128)(2,1)S(1)} collective-permute-done((bf16[24,2304]{1,0:T(8,128)(2,1)S(1)}, bf16[24,2304]{1,0:T(8,128)(2,1)S(1)}, u32[]{:S(2)}, u32[]{:S(2)}) %collective-permute-start.11) | collective-permute-done | bytes 110624 | tf_op jit(solution)/shard_map/ppermute | solution.py:545
  30.5 1.5 %collective-permute-start.18 = (bf16[48,2304]{1,0:T(8,128)(2,1)S(1)}, bf16[48,2304]{1,0:T(8,128)(2,1)S(1)}, u32[]{:S(2)}, u32[]{:S(2)}) collective-permute-start(bf16[48,2304]{1,0:T(8,128)(2,1)S(1)} %get-tuple-element.71), channel_id=1, source_target_pairs={{0,1},{1,0},{2,3},{3,2},{4,6},{5,7},{6,4},{7,5},{8,9},{9,8},{10,11... | collective-permute-start | bytes 663560 | tf_op jit(solution)/shard_map/ppermute | solution.py:553
  32.6 3.9 %collective-permute-done.18 = bf16[48,2304]{1,0:T(8,128)(2,1)S(1)} collective-permute-done((bf16[48,2304]{1,0:T(8,128)(2,1)S(1)}, bf16[48,2304]{1,0:T(8,128)(2,1)S(1)}, u32[]{:S(2)}, u32[]{:S(2)}) %collective-permute-start.18) | collective-permute-done | bytes 221216 | tf_op jit(solution)/shard_map/ppermute | solution.py:553
  36.5 1.6 %collective-permute-start.20 = (bf16[48,2304]{1,0:T(8,128)(2,1)S(1)}, bf16[48,2304]{1,0:T(8,128)(2,1)S(1)}, u32[]{:S(2)}, u32[]{:S(2)}) collective-permute-start(bf16[48,2304]{1,0:T(8,128)(2,1)S(1)} %add.20.kept_second), channel_id=1, source_target_pairs={{0,2},{1,3},{2,0},{3,1},{4,5},{5,4},{6,7},{7,6},{8,10},{9,11},{10,... | collective-permute-start | bytes 663560 | tf_op jit(solution)/shard_map/ppermute | solution.py:553
  39.0 1.6 %collective-permute-start.19 = (bf16[48,2304]{1,0:T(8,128)(2,1)S(1)}, bf16[48,2304]{1,0:T(8,128)(2,1)S(1)}, u32[]{:S(2)}, u32[]{:S(2)}) collective-permute-start(bf16[48,2304]{1,0:T(8,128)(2,1)S(1)} %add.19.kept_first), channel_id=1, source_target_pairs={{0,2},{1,3},{2,0},{3,1},{4,5},{5,4},{6,7},{7,6},{8,10},{9,11},{10,... | collective-permute-start | bytes 663560 | tf_op jit(solution)/shard_map/ppermute | solution.py:553
  42.5 2.5 %collective-permute-done.19.got_first = bf16[48,2304]{1,0:T(8,128)(2,1)S(1)} collective-permute-done((bf16[48,2304]{1,0:T(8,128)(2,1)S(1)}, bf16[48,2304]{1,0:T(8,128)(2,1)S(1)}, u32[]{:S(2)}, u32[]{:S(2)}) %collective-permute-start.19) | collective-permute-done | bytes 221216 | tf_op jit(solution)/shard_map/ppermute | solution.py:553
  45.1 2.7 %shard_map.190 = (f32[12,4608]{1,0:T(8,128)S(1)}, bf16[12,4608]{1,0:T(8,128)(2,1)S(1)}, bf16[24,2304]{1,0:T(8,128)(2,1)S(1)}, bf16[24,2304]{1,0:T(8,128)(2,1)S(1)}, bf16[24,2304]{1,0:T(8,128)(2,1)S(1)}) custom-call(s32[2,2]{1,0:T(2,128)S(1)} %copy-done.6, s32[2,2]{1,0:T(2,128)S(1)} %copy-done.7, s32[2]{0:T(128)S(1)} %copy-done.8, ...), custom_call_target="tpu_custom_call" | custom-call | flops 339738624 | bytes 3397386 | tf_op jit(solution)/shard_map/pallas_call | solution.py:646
  47.8 1.5 %collective-permute-start.21 = (bf16[24,2304]{1,0:T(8,128)(2,1)S(1)}, bf16[24,2304]{1,0:T(8,128)(2,1)S(1)}, u32[]{:S(2)}, u32[]{:S(2)}) collective-permute-start(bf16[24,2304]{1,0:T(8,128)(2,1)S(1)} %get-tuple-element.76), channel_id=1, source_target_pairs={{0,1},{1,0},{2,3},{3,2},{4,5},{5,4},{6,7},{7,6},{8,9},{9,8},{10,11... | collective-permute-start | bytes 331784 | tf_op jit(solution)/shard_map/ppermute | solution.py:676
  49.4 1.5 %collective-permute-start.22 = (bf16[24,2304]{1,0:T(8,128)(2,1)S(1)}, bf16[24,2304]{1,0:T(8,128)(2,1)S(1)}, u32[]{:S(2)}, u32[]{:S(2)}) collective-permute-start(bf16[24,2304]{1,0:T(8,128)(2,1)S(1)} %get-tuple-element.77), channel_id=1, source_target_pairs={{0,2},{1,3},{2,0},{3,1},{4,6},{5,7},{6,4},{7,5},{8,10},{9,11},{10,... | collective-permute-start | bytes 331784 | tf_op jit(solution)/shard_map/ppermute | solution.py:676
  51.4 2.3 %collective-permute-done.21.refs_0_ = bf16[24,2304]{1,0:T(8,128)(2,1)S(1)} collective-permute-done((bf16[24,2304]{1,0:T(8,128)(2,1)S(1)}, bf16[24,2304]{1,0:T(8,128)(2,1)S(1)}, u32[]{:S(2)}, u32[]{:S(2)}) %collective-permute-start.21) | collective-permute-done | bytes 110624 | tf_op jit(solution)/shard_map/ppermute | solution.py:676
  56.9 2.6 %collective-permute-start.29 = (bf16[24,2304]{1,0:T(8,128)(2,1)S(1)}, bf16[24,2304]{1,0:T(8,128)(2,1)S(1)}, u32[]{:S(2)}, u32[]{:S(2)}) collective-permute-start(bf16[24,2304]{1,0:T(8,128)(2,1)S(1)} %shard_map.191.refs_0_), channel_id=1, source_target_pairs={{0,24},{4,28},{8,16},{12,20},{16,8},{20,12},{24,0},{28,4},{1,25},{... | collective-permute-start | bytes 331784 | tf_op jit(solution)/shard_map/ppermute | solution.py:545
  61.4 3.1 %collective-permute-done.29.refs_2_ = bf16[24,2304]{1,0:T(8,128)(2,1)S(1)} collective-permute-done((bf16[24,2304]{1,0:T(8,128)(2,1)S(1)}, bf16[24,2304]{1,0:T(8,128)(2,1)S(1)}, u32[]{:S(2)}, u32[]{:S(2)}) %collective-permute-start.29) | collective-permute-done | bytes 110624 | tf_op jit(solution)/shard_map/ppermute | solution.py:545
  64.5 3.6 %collective-permute-done.28.refs_1_ = bf16[24,2304]{1,0:T(8,128)(2,1)S(1)} collective-permute-done((bf16[24,2304]{1,0:T(8,128)(2,1)S(1)}, bf16[24,2304]{1,0:T(8,128)(2,1)S(1)}, u32[]{:S(2)}, u32[]{:S(2)}) %collective-permute-start.28) | collective-permute-done | bytes 110624 | tf_op jit(solution)/shard_map/ppermute | solution.py:545
  68.7 8.4 %collective-permute-done.30.refs_1_ = bf16[72,2304]{1,0:T(8,128)(2,1)S(1)} collective-permute-done((bf16[72,2304]{1,0:T(8,128)(2,1)S(1)}, bf16[72,2304]{1,0:T(8,128)(2,1)S(1)}, u32[]{:S(2)}, u32[]{:S(2)}) %collective-permute-start.30) | collective-permute-done | bytes 331808 | tf_op jit(solution)/shard_map/ppermute | solution.py:553
  79.5 7.0 %collective-permute-done.35.refs_2_ = bf16[24,2304]{1,0:T(8,128)(2,1)S(1)} collective-permute-done((bf16[24,2304]{1,0:T(8,128)(2,1)S(1)}, bf16[24,2304]{1,0:T(8,128)(2,1)S(1)}, u32[]{:S(2)}, u32[]{:S(2)}) %collective-permute-start.35) | collective-permute-done | bytes 110624 | tf_op jit(solution)/shard_map/ppermute | solution.py:553
  89.4 3.7 %collective-permute-done.25.refs_0_ = bf16[24,2304]{1,0:T(8,128)(2,1)S(1)} collective-permute-done((bf16[24,2304]{1,0:T(8,128)(2,1)S(1)}, bf16[24,2304]{1,0:T(8,128)(2,1)S(1)}, u32[]{:S(2)}, u32[]{:S(2)}) %collective-permute-start.25) | collective-permute-done | bytes 110624 | tf_op jit(solution)/shard_map/ppermute | solution.py:553
  96.6 1.6 %shard_map.194.refs_6_ = f32[12,48]{1,0:T(8,128)S(1)} custom-call(bf16[24,2304]{1,0:T(8,128)(2,1)S(1)} %collective-permute-done.24.refs_0_, bf16[72,2304]{1,0:T(8,128)(2,1)S(1)} %collective-permute-done.30.refs_1_, bf16[24,2304]{1,0:T(8,128)(2,1)S(1)} %collective-permute-done.35.refs_2_, bf16[72,2304]{1,0:T(8,128)(2,1)S(1)} %collective-permute-done.36.refs_3_, ...), custom_call_target="tpu_custom_call" | custom-call | flops 905969664 | bytes 9059696 | tf_op jit(solution)/shard_map/pallas_call | solution.py:717
  99.8 11.3 %all_to_all.11 = f32[32,4,128]{2,1,0:T(4,128)S(1)} all-to-all(f32[32,4,128]{2,1,0:T(4,128)S(1)} %bitcast.4), channel_id=1, replica_groups=mesh['batch'=8,'vocab'=4] {'batch','vocab'}, dimensions={0} | all-to-all | bytes 131072 | tf_op jit(solution)/shard_map/all_to_all | solution.py:743
  (98 shorter events, 30.2 us)
Async XLA Ops:
  15.2 5.8 %collective-permute-start.10 = (bf16[24,2304]{1,0:T(8,128)(2,1)S(1)}, bf16[24,2304]{1,0:T(8,128)(2,1)S(1)}, u32[]{:S(2)}, u32[]{:S(2)}) collective-permute-start(bf16[24,2304]{1,0:T(8,128)(2,1)S(1)} %get-tuple-element.64), channel_id=1, source_target_pairs={{0,8},{4,12},{8,0},{12,4},{16,24},{20,28},{24,16},{28,20},{1,9},{5... | collective-permute-start | bytes 331784 | tf_op jit(solution)/shard_map/ppermute | solution.py:545
  17.2 9.8 %collective-permute-start.11 = (bf16[24,2304]{1,0:T(8,128)(2,1)S(1)}, bf16[24,2304]{1,0:T(8,128)(2,1)S(1)}, u32[]{:S(2)}, u32[]{:S(2)}) collective-permute-start(bf16[24,2304]{1,0:T(8,128)(2,1)S(1)} %get-tuple-element.65), channel_id=1, source_target_pairs={{0,16},{4,20},{8,24},{12,28},{16,0},{20,4},{24,8},{28,12},{1,17},{... | collective-permute-start | bytes 331784 | tf_op jit(solution)/shard_map/ppermute | solution.py:545
  19.9 7.1 %collective-permute-start.12 = (bf16[24,2304]{1,0:T(8,128)(2,1)S(1)}, bf16[24,2304]{1,0:T(8,128)(2,1)S(1)}, u32[]{:S(2)}, u32[]{:S(2)}) collective-permute-start(bf16[24,2304]{1,0:T(8,128)(2,1)S(1)} %get-tuple-element.66), channel_id=1, source_target_pairs={{0,24},{4,28},{8,16},{12,20},{16,8},{20,12},{24,0},{28,4},{1,25},{... | collective-permute-start | bytes 331784 | tf_op jit(solution)/shard_map/ppermute | solution.py:545
  19.9 7.6 %collective-permute-start.13 = (bf16[24,2304]{1,0:T(8,128)(2,1)S(1)}, bf16[24,2304]{1,0:T(8,128)(2,1)S(1)}, u32[]{:S(2)}, u32[]{:S(2)}) collective-permute-start(bf16[24,2304]{1,0:T(8,128)(2,1)S(1)} %get-tuple-element.63.refs_1_), channel_id=1, source_target_pairs={{0,4},{4,0},{8,12},{12,8},{16,20},{20,16},{24,28},{28,24},{1,5},{5... | collective-permute-start | bytes 331784 | tf_op jit(solution)/shard_map/ppermute | solution.py:545
  21.0 6.5 %collective-permute-start.14 = (bf16[24,2304]{1,0:T(8,128)(2,1)S(1)}, bf16[24,2304]{1,0:T(8,128)(2,1)S(1)}, u32[]{:S(2)}, u32[]{:S(2)}) collective-permute-start(bf16[24,2304]{1,0:T(8,128)(2,1)S(1)} %collective-permute-done.10.refs_2_), channel_id=1, source_target_pairs={{0,4},{4,0},{8,12},{12,8},{16,20},{20,16},{24,28},{28,24},{1,5},{5... | collective-permute-start | bytes 331784 | tf_op jit(solution)/shard_map/ppermute | solution.py:545
  30.5 6.0 %collective-permute-start.18 = (bf16[48,2304]{1,0:T(8,128)(2,1)S(1)}, bf16[48,2304]{1,0:T(8,128)(2,1)S(1)}, u32[]{:S(2)}, u32[]{:S(2)}) collective-permute-start(bf16[48,2304]{1,0:T(8,128)(2,1)S(1)} %get-tuple-element.71), channel_id=1, source_target_pairs={{0,1},{1,0},{2,3},{3,2},{4,6},{5,7},{6,4},{7,5},{8,9},{9,8},{10,11... | collective-permute-start | bytes 663560 | tf_op jit(solution)/shard_map/ppermute | solution.py:553
  32.0 7.0 %collective-permute-start.17 = (bf16[48,2304]{1,0:T(8,128)(2,1)S(1)}, bf16[48,2304]{1,0:T(8,128)(2,1)S(1)}, u32[]{:S(2)}, u32[]{:S(2)}) collective-permute-start(bf16[48,2304]{1,0:T(8,128)(2,1)S(1)} %get-tuple-element.70), channel_id=1, source_target_pairs={{0,1},{1,0},{2,3},{3,2},{4,6},{5,7},{6,4},{7,5},{8,9},{9,8},{10,11... | collective-permute-start | bytes 663560 | tf_op jit(solution)/shard_map/ppermute | solution.py:553
  36.5 6.0 %collective-permute-start.20 = (bf16[48,2304]{1,0:T(8,128)(2,1)S(1)}, bf16[48,2304]{1,0:T(8,128)(2,1)S(1)}, u32[]{:S(2)}, u32[]{:S(2)}) collective-permute-start(bf16[48,2304]{1,0:T(8,128)(2,1)S(1)} %add.20.kept_second), channel_id=1, source_target_pairs={{0,2},{1,3},{2,0},{3,1},{4,5},{5,4},{6,7},{7,6},{8,10},{9,11},{10,... | collective-permute-start | bytes 663560 | tf_op jit(solution)/shard_map/ppermute | solution.py:553
  39.0 6.0 %collective-permute-start.19 = (bf16[48,2304]{1,0:T(8,128)(2,1)S(1)}, bf16[48,2304]{1,0:T(8,128)(2,1)S(1)}, u32[]{:S(2)}, u32[]{:S(2)}) collective-permute-start(bf16[48,2304]{1,0:T(8,128)(2,1)S(1)} %add.19.kept_first), channel_id=1, source_target_pairs={{0,2},{1,3},{2,0},{3,1},{4,5},{5,4},{6,7},{7,6},{8,10},{9,11},{10,... | collective-permute-start | bytes 663560 | tf_op jit(solution)/shard_map/ppermute | solution.py:553
  47.8 5.9 %collective-permute-start.21 = (bf16[24,2304]{1,0:T(8,128)(2,1)S(1)}, bf16[24,2304]{1,0:T(8,128)(2,1)S(1)}, u32[]{:S(2)}, u32[]{:S(2)}) collective-permute-start(bf16[24,2304]{1,0:T(8,128)(2,1)S(1)} %get-tuple-element.76), channel_id=1, source_target_pairs={{0,1},{1,0},{2,3},{3,2},{4,5},{5,4},{6,7},{7,6},{8,9},{9,8},{10,11... | collective-permute-start | bytes 331784 | tf_op jit(solution)/shard_map/ppermute | solution.py:676
  49.4 5.7 %collective-permute-start.22 = (bf16[24,2304]{1,0:T(8,128)(2,1)S(1)}, bf16[24,2304]{1,0:T(8,128)(2,1)S(1)}, u32[]{:S(2)}, u32[]{:S(2)}) collective-permute-start(bf16[24,2304]{1,0:T(8,128)(2,1)S(1)} %get-tuple-element.77), channel_id=1, source_target_pairs={{0,2},{1,3},{2,0},{3,1},{4,6},{5,7},{6,4},{7,5},{8,10},{9,11},{10,... | collective-permute-start | bytes 331784 | tf_op jit(solution)/shard_map/ppermute | solution.py:676
  56.9 7.5 %collective-permute-start.29 = (bf16[24,2304]{1,0:T(8,128)(2,1)S(1)}, bf16[24,2304]{1,0:T(8,128)(2,1)S(1)}, u32[]{:S(2)}, u32[]{:S(2)}) collective-permute-start(bf16[24,2304]{1,0:T(8,128)(2,1)S(1)} %shard_map.191.refs_0_), channel_id=1, source_target_pairs={{0,24},{4,28},{8,16},{12,20},{16,8},{20,12},{24,0},{28,4},{1,25},{... | collective-permute-start | bytes 331784 | tf_op jit(solution)/shard_map/ppermute | solution.py:545
  59.5 8.6 %collective-permute-start.28 = (bf16[24,2304]{1,0:T(8,128)(2,1)S(1)}, bf16[24,2304]{1,0:T(8,128)(2,1)S(1)}, u32[]{:S(2)}, u32[]{:S(2)}) collective-permute-start(bf16[24,2304]{1,0:T(8,128)(2,1)S(1)} %shard_map.191.refs_0_), channel_id=1, source_target_pairs={{0,16},{4,20},{8,24},{12,28},{16,0},{20,4},{24,8},{28,12},{1,17},{... | collective-permute-start | bytes 331784 | tf_op jit(solution)/shard_map/ppermute | solution.py:545
  60.3 7.8 %collective-permute-start.27 = (bf16[24,2304]{1,0:T(8,128)(2,1)S(1)}, bf16[24,2304]{1,0:T(8,128)(2,1)S(1)}, u32[]{:S(2)}, u32[]{:S(2)}) collective-permute-start(bf16[24,2304]{1,0:T(8,128)(2,1)S(1)} %shard_map.191.refs_0_), channel_id=1, source_target_pairs={{0,8},{4,12},{8,0},{12,4},{16,24},{20,28},{24,16},{28,20},{1,9},{5... | collective-permute-start | bytes 331784 | tf_op jit(solution)/shard_map/ppermute | solution.py:545
  68.1 8.9 %collective-permute-start.30 = (bf16[72,2304]{1,0:T(8,128)(2,1)S(1)}, bf16[72,2304]{1,0:T(8,128)(2,1)S(1)}, u32[]{:S(2)}, u32[]{:S(2)}) collective-permute-start(bf16[72,2304]{1,0:T(8,128)(2,1)S(1)} %shard_map.192.refs_1_), channel_id=1, source_target_pairs={{0,2},{1,3},{2,0},{3,1},{4,5},{5,4},{6,7},{7,6},{8,10},{9,11},{10,... | collective-permute-start | bytes 995336 | tf_op jit(solution)/shard_map/ppermute | solution.py:553
  68.7 18.4 %collective-permute-start.36 = (bf16[72,2304]{1,0:T(8,128)(2,1)S(1)}, bf16[72,2304]{1,0:T(8,128)(2,1)S(1)}, u32[]{:S(2)}, u32[]{:S(2)}) collective-permute-start(bf16[72,2304]{1,0:T(8,128)(2,1)S(1)} %shard_map.192.refs_1_), channel_id=1, source_target_pairs={{0,1},{1,0},{2,3},{3,2},{4,6},{5,7},{6,4},{7,5},{8,9},{9,8},{10,11... | collective-permute-start | bytes 995336 | tf_op jit(solution)/shard_map/ppermute | solution.py:553
  77.1 10.5 %collective-permute-start.31 = (bf16[72,2304]{1,0:T(8,128)(2,1)S(1)}, bf16[72,2304]{1,0:T(8,128)(2,1)S(1)}, u32[]{:S(2)}, u32[]{:S(2)}) collective-permute-start(bf16[72,2304]{1,0:T(8,128)(2,1)S(1)} %collective-permute-done.30.refs_1_), channel_id=1, source_target_pairs={{0,1},{1,0},{2,3},{3,2},{4,6},{5,7},{6,4},{7,5},{8,9},{9,8},{10,11... | collective-permute-start | bytes 995336 | tf_op jit(solution)/shard_map/ppermute | solution.py:553
  78.1 8.4 %collective-permute-start.35 = (bf16[24,2304]{1,0:T(8,128)(2,1)S(1)}, bf16[24,2304]{1,0:T(8,128)(2,1)S(1)}, u32[]{:S(2)}, u32[]{:S(2)}) collective-permute-start(bf16[24,2304]{1,0:T(8,128)(2,1)S(1)} %shard_map.191.refs_0_), channel_id=1, source_target_pairs={{0,1},{1,0},{2,3},{3,2},{4,6},{5,7},{6,4},{7,5},{8,9},{9,8},{10,11... | collective-permute-start | bytes 331784 | tf_op jit(solution)/shard_map/ppermute | solution.py:553
  79.1 7.5 %collective-permute-start.33 = (bf16[24,2304]{1,0:T(8,128)(2,1)S(1)}, bf16[24,2304]{1,0:T(8,128)(2,1)S(1)}, u32[]{:S(2)}, u32[]{:S(2)}) collective-permute-start(bf16[24,2304]{1,0:T(8,128)(2,1)S(1)} %shard_map.191.refs_0_), channel_id=1, source_target_pairs={{0,4},{4,0},{8,12},{12,8},{16,20},{20,16},{24,28},{28,24},{1,5},{5... | collective-permute-start | bytes 331784 | tf_op jit(solution)/shard_map/ppermute | solution.py:545
  79.1 8.1 %collective-permute-start.24 = (bf16[24,2304]{1,0:T(8,128)(2,1)S(1)}, bf16[24,2304]{1,0:T(8,128)(2,1)S(1)}, u32[]{:S(2)}, u32[]{:S(2)}) collective-permute-start(bf16[24,2304]{1,0:T(8,128)(2,1)S(1)} %shard_map.191.refs_0_), channel_id=1, source_target_pairs={{0,2},{1,3},{2,0},{3,1},{4,5},{5,4},{6,7},{7,6},{8,10},{9,11},{10,... | collective-permute-start | bytes 331784 | tf_op jit(solution)/shard_map/ppermute | solution.py:553
  86.5 6.5 %collective-permute-start.34 = (bf16[72,2304]{1,0:T(8,128)(2,1)S(1)}, bf16[72,2304]{1,0:T(8,128)(2,1)S(1)}, u32[]{:S(2)}, u32[]{:S(2)}) collective-permute-start(bf16[72,2304]{1,0:T(8,128)(2,1)S(1)} %shard_map.192.refs_1_), channel_id=1, source_target_pairs={{0,4},{4,0},{8,12},{12,8},{16,20},{20,16},{24,28},{28,24},{1,5},{5... | collective-permute-start | bytes 995336 | tf_op jit(solution)/shard_map/ppermute | solution.py:545
  87.1 9.5 %collective-permute-start.40 = (bf16[72,2304]{1,0:T(8,128)(2,1)S(1)}, bf16[72,2304]{1,0:T(8,128)(2,1)S(1)}, u32[]{:S(2)}, u32[]{:S(2)}) collective-permute-start(bf16[72,2304]{1,0:T(8,128)(2,1)S(1)} %collective-permute-done.36.refs_3_), channel_id=1, source_target_pairs={{0,4},{4,0},{8,12},{12,8},{16,20},{20,16},{24,28},{28,24},{1,5},{5... | collective-permute-start | bytes 995336 | tf_op jit(solution)/shard_map/ppermute | solution.py:545
  87.1 9.4 %collective-permute-start.38 = (bf16[72,2304]{1,0:T(8,128)(2,1)S(1)}, bf16[72,2304]{1,0:T(8,128)(2,1)S(1)}, u32[]{:S(2)}, u32[]{:S(2)}) collective-permute-start(bf16[72,2304]{1,0:T(8,128)(2,1)S(1)} %collective-permute-done.30.refs_1_), channel_id=1, source_target_pairs={{0,4},{4,0},{8,12},{12,8},{16,20},{20,16},{24,28},{28,24},{1,5},{5... | collective-permute-start | bytes 995336 | tf_op jit(solution)/shard_map/ppermute | solution.py:545
  87.6 10.6 %collective-permute-start.32 = (bf16[72,2304]{1,0:T(8,128)(2,1)S(1)}, bf16[72,2304]{1,0:T(8,128)(2,1)S(1)}, u32[]{:S(2)}, u32[]{:S(2)}) collective-permute-start(bf16[72,2304]{1,0:T(8,128)(2,1)S(1)} %collective-permute-done.31.refs_1_), channel_id=1, source_target_pairs={{0,4},{4,0},{8,12},{12,8},{16,20},{20,16},{24,28},{28,24},{1,5},{5... | collective-permute-start | bytes 995336 | tf_op jit(solution)/shard_map/ppermute | solution.py:545
  (25 other events, 213.6 us)

commit v3 on v2

--- a/solution.py
+++ b/solution.py
@@ -342,16 +342,16 @@
     joint[...] = jnp.concatenate([part[...].astype(f32) for part in parts], axis=0).astype(bf16)
 
 
-def half_of_block(near, distant, half):
-    size = near.shape[0]
+def half_of_block(parts, half):
+    size = parts[0].shape[0]
     chunk = size // half_count
-    count = distant.shape[0] // size
-    parts = [near[...].astype(f32)[half * chunk : (half + 1) * chunk]]
-    values = distant[...].astype(f32)
-    for at in range(count):
-        start = at * size + half * chunk
-        parts.append(values[start : start + chunk])
-    return jnp.concatenate(parts, axis=0)
+    found = []
+    for part in parts:
+        values = part[...].astype(f32)
+        for at in range(part.shape[0] // size):
+            start = at * size + half * chunk
+            found.append(values[start : start + chunk])
+    return jnp.concatenate(found, axis=0)
 
 
 def score_blocks(blocks, core_of, order_of, tables, pools):
@@ -378,7 +378,7 @@
         wanted.append(jnp.concatenate(parts, axis=1))
     wanted = jnp.concatenate(wanted, axis=1) - first
     values = [
-        jnp.concatenate([half_of_block(*block, half) for block in blocks], axis=0).astype(bf16)
+        jnp.concatenate([half_of_block(block, half) for block in blocks], axis=0).astype(bf16)
         for half in range(half_count)
     ]
     wide = values[0].shape[1]
@@ -423,14 +423,14 @@
             scores[row : row + 1, :] = found[kind][at]
 
 
-def late_kernel(orders, *refs):
+def late_kernel(orders, halves, *refs):
     vocab_devices = lax.axis_size("vocab")
     at_vocab = lax.axis_index("vocab")
     at_batch = lax.axis_index("batch")
     far = lax.axis_size("batch") // 2
     message = refs[-1]
     scores = refs[-2 - len(orders) : -1]
-    block, tables, pools = refs[:2], refs[2:4], refs[4]
+    block, tables, pools = refs[:halves], refs[halves : halves + 2], refs[halves + 2]
     chunk = block[0].shape[0] // half_count
     late = score_blocks([block], [1], [vocab_devices - 1], tables, pools)
     for other in range(2):
@@ -562,7 +562,7 @@
             pltpu.VMEM((2, iter_count, local_batch, width), jnp.int32),
             pltpu.SemaphoreType.DMA((2,)),
         ],
-        grant=60,
+        grant=2,
     )(window_ids, pool_ids)
     all_ids = own_ids
     for bit in bits_of(batch_devices):
@@ -686,13 +686,13 @@
         parts.append(batch_swap(final, 2 * mask))
     joint = call(
         join_kernel,
-        shape((far - 1) * half_count * chunk, model_width // half_count),
-        [vmem] * (far - 1),
+        shape((far - 2) * half_count * chunk, model_width // half_count),
+        [vmem] * (far - 2),
         vmem,
-    )(*parts)
-    halves = 2
+    )(*parts[1:])
+    halves = 3
     own_blocks, other_blocks = [], []
-    for block in (final, joint):
+    for block in (final, parts[0], joint):
         blocks = [block]
         for step in range(len(vocab_bits)):
             step = len(vocab_bits) - 1 - step
@@ -734,7 +734,7 @@
         )(*halves_of(own_blocks, [last]), *tables, pools)
     )
     message = call(
-        functools.partial(late_kernel, groups_of),
+        functools.partial(late_kernel, groups_of, halves),
         shape(all_devices * vocab_devices, lane_count, kind=f32),
         [vmem] * (halves + 3 + len(scores)),
         vmem,

time: 112 us -> 107 us (0.955)
  waiting for transfers between devices: 49.2 us -> 41.5 us
  starting transfers between devices: 30.8 us -> 34.4 us
  local copies, waits for them, and re-layouts: 0.14 us -> 1.49 us
  Pallas kernels: 17.5 us -> 16.2 us
    ppermute x10 -> x13, waiting for transfers between devices: 27.5 us -> 21.3 us  [mixed_swap(): return lax.ppermute(value, ('batch', 'vocab'), pairs)]
    ppermute x10 -> x13, starting transfers between devices: 9.39 us -> 12.3 us  [mixed_swap(): return lax.ppermute(value, ('batch', 'vocab'), pairs)]
    ppermute x21 -> x25, waiting for transfers between devices: 16.6 us -> 15.1 us  [batch_swap(): lax.ppermute(value, 'batch', [(at, at ^ mask) for at in range(batch_devic...]
    unnamed x30 -> x32, local copies, waits for them, and re-layouts: 0.09 us -> 1.45 us
    pallas_call x1, Pallas kernels: 1.31 us -> 0.03 us  [per_device(): call(pack_kernel, shape(2 * groups, width, kind=jnp.int32), [in_hbm] * 2,...]
    ppermute x21 -> x25, starting transfers between devices: 17.9 us -> 18.5 us  [batch_swap(): lax.ppermute(value, 'batch', [(at, at ^ mask) for at in range(batch_devic...]
  transfers between devices with their start and end apart: 34 -> 41, of which waited for: 19 -> 20; matrix products, arithmetic and copies ran while one was open for 0% -> 0% of each run, Pallas kernels for 8% -> 8%
where the time goes in v3:
time: 107 us
  waiting for transfers between devices  41.5 us (39%)
  starting transfers between devices  34.4 us (32%)
  Pallas kernels  16.2 us (15%)
  blocking collectives  11.3 us (11%)
  local copies, waits for them, and re-layouts  1.49 us (1%)
    ppermute x13, waiting for transfers between devices, mixed_swap(): return lax.ppermute(value, ('batch', 'vocab'), pairs)  21.3 us
    ppermute x25, starting transfers between devices, batch_swap(): lax.ppermute(value, 'batch', [(at, at ^ mask) for at in range(batch_devic...  18.5 us
    ppermute x25, waiting for transfers between devices, batch_swap(): lax.ppermute(value, 'batch', [(at, at ^ mask) for at in range(batch_devic...  15.1 us
    ppermute x13, starting transfers between devices, mixed_swap(): return lax.ppermute(value, ('batch', 'vocab'), pairs)  12.3 us
    all_to_all x1, blocking collectives, per_device(): totals = lax.all_to_all(message, ('batch', 'vocab'), 0, 0, tiled=True)  11.3 us
    ppermute x3, waiting for transfers between devices, per_device(): branches.append(lax.ppermute(send, 'vocab', pairs))  5.12 us
    ppermute x3, starting transfers between devices, per_device(): branches.append(lax.ppermute(send, 'vocab', pairs))  3.55 us
    pallas_call x2, Pallas kernels, per_device(): call(functools.partial(load_kernel, at * part_rows), shape(part_rows, mod...  3.35 us
  transfers between devices with their start and end apart: 41, of which 20 were waited for; matrix products, arithmetic and copies ran while one was open for 0% of the time, Pallas kernels for 8%

profile of v3, /device:TPU:0, one launch (start us, length us, event | category | flops | bytes accessed | tf_op | source)
XLA Modules:
  0.0 107.1 jit_solution(16273842586388673166)
XLA Ops:
  3.4 3.0 %collective-permute-start.8 = (s32[24,8]{1,0:T(8,128)S(1)}, s32[24,8]{1,0:T(8,128)S(1)}, u32[]{:S(2)}, u32[]{:S(2)}) collective-permute-start(s32[24,8]{1,0:T(8,128)S(1)} %pad_add_fusion.2), channel_id=1, source_target_pairs={{0,8},{4,12},{8,0},{12,4},{16,24},{20,28},{24,16},{28,20},{1,9},{5... | collective-permute-start | bytes 2312 | tf_op jit(solution)/shard_map/ppermute | solution.py:545
  6.4 1.7 %shard_map.186.lower.refs_7_.refs_13_.refs_4_ = bf16[256,4608]{1,0:T(8,128)(2,1)S(1)} custom-call(bf16[512,4608]{1,0:T(8,128)(2,1)} %source.3), custom_call_target="tpu_custom_call" | custom-call | flops 100000000 | bytes 1000000 | tf_op jit(solution)/shard_map/pallas_call | solution.py:575
  8.1 3.1 %collective-permute-start.9 = (s32[48,8]{1,0:T(8,128)S(1)}, s32[48,8]{1,0:T(8,128)S(1)}, u32[]{:S(2)}, u32[]{:S(2)}) collective-permute-start(s32[48,8]{1,0:T(8,128)S(1)} %pad_add_fusion.1), channel_id=1, source_target_pairs={{0,16},{4,20},{8,24},{12,28},{16,0},{20,4},{24,8},{28,12},{1,17},{... | collective-permute-start | bytes 4616 | tf_op jit(solution)/shard_map/ppermute | solution.py:545
  11.2 1.7 %shard_map.185.upper.refs_6_.refs_12_.refs_3_ = bf16[256,4608]{1,0:T(8,128)(2,1)S(1)} custom-call(bf16[512,4608]{1,0:T(8,128)(2,1)} %source.3), custom_call_target="tpu_custom_call" | custom-call | flops 100000000 | bytes 1000000 | tf_op jit(solution)/shard_map/pallas_call | solution.py:575
  14.4 2.0 %collective-permute-start.10 = (bf16[24,2304]{1,0:T(8,128)(2,1)S(1)}, bf16[24,2304]{1,0:T(8,128)(2,1)S(1)}, u32[]{:S(2)}, u32[]{:S(2)}) collective-permute-start(bf16[24,2304]{1,0:T(8,128)(2,1)S(1)} %get-tuple-element.64), channel_id=1, source_target_pairs={{0,8},{4,12},{8,0},{12,4},{16,24},{20,28},{24,16},{28,20},{1,9},{5... | collective-permute-start | bytes 331784 | tf_op jit(solution)/shard_map/ppermute | solution.py:545
  16.4 2.7 %collective-permute-start.11 = (bf16[24,2304]{1,0:T(8,128)(2,1)S(1)}, bf16[24,2304]{1,0:T(8,128)(2,1)S(1)}, u32[]{:S(2)}, u32[]{:S(2)}) collective-permute-start(bf16[24,2304]{1,0:T(8,128)(2,1)S(1)} %get-tuple-element.65), channel_id=1, source_target_pairs={{0,16},{4,20},{8,24},{12,28},{16,0},{20,4},{24,8},{28,12},{1,17},{... | collective-permute-start | bytes 331784 | tf_op jit(solution)/shard_map/ppermute | solution.py:545
  20.1 6.0 %collective-permute-done.11.refs_3_ = bf16[24,2304]{1,0:T(8,128)(2,1)S(1)} collective-permute-done((bf16[24,2304]{1,0:T(8,128)(2,1)S(1)}, bf16[24,2304]{1,0:T(8,128)(2,1)S(1)}, u32[]{:S(2)}, u32[]{:S(2)}) %collective-permute-start.11) | collective-permute-done | bytes 110624 | tf_op jit(solution)/shard_map/ppermute | solution.py:545
  31.7 3.9 %collective-permute-done.18 = bf16[48,2304]{1,0:T(8,128)(2,1)S(1)} collective-permute-done((bf16[48,2304]{1,0:T(8,128)(2,1)S(1)}, bf16[48,2304]{1,0:T(8,128)(2,1)S(1)}, u32[]{:S(2)}, u32[]{:S(2)}) %collective-permute-start.18) | collective-permute-done | bytes 221216 | tf_op jit(solution)/shard_map/ppermute | solution.py:553
  35.6 1.6 %collective-permute-start.20 = (bf16[48,2304]{1,0:T(8,128)(2,1)S(1)}, bf16[48,2304]{1,0:T(8,128)(2,1)S(1)}, u32[]{:S(2)}, u32[]{:S(2)}) collective-permute-start(bf16[48,2304]{1,0:T(8,128)(2,1)S(1)} %add.20.kept_second), channel_id=1, source_target_pairs={{0,2},{1,3},{2,0},{3,1},{4,5},{5,4},{6,7},{7,6},{8,10},{9,11},{10,... | collective-permute-start | bytes 663560 | tf_op jit(solution)/shard_map/ppermute | solution.py:553
  38.2 1.6 %collective-permute-start.19 = (bf16[48,2304]{1,0:T(8,128)(2,1)S(1)}, bf16[48,2304]{1,0:T(8,128)(2,1)S(1)}, u32[]{:S(2)}, u32[]{:S(2)}) collective-permute-start(bf16[48,2304]{1,0:T(8,128)(2,1)S(1)} %add.19.kept_first), channel_id=1, source_target_pairs={{0,2},{1,3},{2,0},{3,1},{4,5},{5,4},{6,7},{7,6},{8,10},{9,11},{10,... | collective-permute-start | bytes 663560 | tf_op jit(solution)/shard_map/ppermute | solution.py:553
  41.6 2.5 %collective-permute-done.19.got_first = bf16[48,2304]{1,0:T(8,128)(2,1)S(1)} collective-permute-done((bf16[48,2304]{1,0:T(8,128)(2,1)S(1)}, bf16[48,2304]{1,0:T(8,128)(2,1)S(1)}, u32[]{:S(2)}, u32[]{:S(2)}) %collective-permute-start.19) | collective-permute-done | bytes 221216 | tf_op jit(solution)/shard_map/ppermute | solution.py:553
  44.2 2.7 %shard_map.190 = (f32[12,4608]{1,0:T(8,128)S(1)}, bf16[12,4608]{1,0:T(8,128)(2,1)S(1)}, bf16[24,2304]{1,0:T(8,128)(2,1)S(1)}, bf16[24,2304]{1,0:T(8,128)(2,1)S(1)}, bf16[24,2304]{1,0:T(8,128)(2,1)S(1)}) custom-call(s32[2,2]{1,0:T(2,128)S(1)} %copy-done.8, s32[2,2]{1,0:T(2,128)S(1)} %copy-done.9, s32[2]{0:T(128)S(1)} %copy-done.10, ...), custom_call_target="tpu_custom_call" | custom-call | flops 339738624 | bytes 3397386 | tf_op jit(solution)/shard_map/pallas_call | solution.py:646
  46.9 1.6 %collective-permute-start.21 = (bf16[24,2304]{1,0:T(8,128)(2,1)S(1)}, bf16[24,2304]{1,0:T(8,128)(2,1)S(1)}, u32[]{:S(2)}, u32[]{:S(2)}) collective-permute-start(bf16[24,2304]{1,0:T(8,128)(2,1)S(1)} %get-tuple-element.76), channel_id=1, source_target_pairs={{0,1},{1,0},{2,3},{3,2},{4,5},{5,4},{6,7},{7,6},{8,9},{9,8},{10,11... | collective-permute-start | bytes 331784 | tf_op jit(solution)/shard_map/ppermute | solution.py:676
  50.5 2.3 %collective-permute-done.21.refs_0_ = bf16[24,2304]{1,0:T(8,128)(2,1)S(1)} collective-permute-done((bf16[24,2304]{1,0:T(8,128)(2,1)S(1)}, bf16[24,2304]{1,0:T(8,128)(2,1)S(1)}, u32[]{:S(2)}, u32[]{:S(2)}) %collective-permute-start.21) | collective-permute-done | bytes 110624 | tf_op jit(solution)/shard_map/ppermute | solution.py:676
  56.0 2.6 %collective-permute-start.32 = (bf16[24,2304]{1,0:T(8,128)(2,1)S(1)}, bf16[24,2304]{1,0:T(8,128)(2,1)S(1)}, u32[]{:S(2)}, u32[]{:S(2)}) collective-permute-start(bf16[24,2304]{1,0:T(8,128)(2,1)S(1)} %shard_map.191.refs_0_), channel_id=1, source_target_pairs={{0,24},{4,28},{8,16},{12,20},{16,8},{20,12},{24,0},{28,4},{1,25},{... | collective-permute-start | bytes 331784 | tf_op jit(solution)/shard_map/ppermute | solution.py:545
  61.0 2.7 %collective-permute-done.32.refs_1_ = bf16[24,2304]{1,0:T(8,128)(2,1)S(1)} collective-permute-done((bf16[24,2304]{1,0:T(8,128)(2,1)S(1)}, bf16[24,2304]{1,0:T(8,128)(2,1)S(1)}, u32[]{:S(2)}, u32[]{:S(2)}) %collective-permute-start.32) | collective-permute-done | bytes 110624 | tf_op jit(solution)/shard_map/ppermute | solution.py:545
  63.8 3.4 %collective-permute-done.31.refs_0_ = bf16[24,2304]{1,0:T(8,128)(2,1)S(1)} collective-permute-done((bf16[24,2304]{1,0:T(8,128)(2,1)S(1)}, bf16[24,2304]{1,0:T(8,128)(2,1)S(1)}, u32[]{:S(2)}, u32[]{:S(2)}) %collective-permute-start.31) | collective-permute-done | bytes 110624 | tf_op jit(solution)/shard_map/ppermute | solution.py:545
  70.1 5.9 %collective-permute-done.24.refs_0_ = bf16[24,2304]{1,0:T(8,128)(2,1)S(1)} collective-permute-done((bf16[24,2304]{1,0:T(8,128)(2,1)S(1)}, bf16[24,2304]{1,0:T(8,128)(2,1)S(1)}, u32[]{:S(2)}, u32[]{:S(2)}) %collective-permute-start.24) | collective-permute-done | bytes 110624 | tf_op jit(solution)/shard_map/ppermute | solution.py:553
  76.5 2.1 %collective-permute-start.25 = (bf16[24,2304]{1,0:T(8,128)(2,1)S(1)}, bf16[24,2304]{1,0:T(8,128)(2,1)S(1)}, u32[]{:S(2)}, u32[]{:S(2)}) collective-permute-start(bf16[24,2304]{1,0:T(8,128)(2,1)S(1)} %collective-permute-done.24.refs_0_), channel_id=1, source_target_pairs={{0,1},{1,0},{2,3},{3,2},{4,6},{5,7},{6,4},{7,5},{8,9},{9,8},{10,11... | collective-permute-start | bytes 331784 | tf_op jit(solution)/shard_map/ppermute | solution.py:553
  78.7 3.2 %collective-permute-done.28.refs_1_ = bf16[24,2304]{1,0:T(8,128)(2,1)S(1)} collective-permute-done((bf16[24,2304]{1,0:T(8,128)(2,1)S(1)}, bf16[24,2304]{1,0:T(8,128)(2,1)S(1)}, u32[]{:S(2)}, u32[]{:S(2)}) %collective-permute-start.28) | collective-permute-done | bytes 110624 | tf_op jit(solution)/shard_map/ppermute | solution.py:553
  83.7 1.7 %collective-permute-start.29 = (bf16[24,2304]{1,0:T(8,128)(2,1)S(1)}, bf16[24,2304]{1,0:T(8,128)(2,1)S(1)}, u32[]{:S(2)}, u32[]{:S(2)}) collective-permute-start(bf16[24,2304]{1,0:T(8,128)(2,1)S(1)} %collective-permute-done.28.refs_1_), channel_id=1, source_target_pairs={{0,1},{1,0},{2,3},{3,2},{4,6},{5,7},{6,4},{7,5},{8,9},{9,8},{10,11... | collective-permute-start | bytes 331784 | tf_op jit(solution)/shard_map/ppermute | solution.py:553
  85.4 3.0 %collective-permute-done.29.refs_1_ = bf16[24,2304]{1,0:T(8,128)(2,1)S(1)} collective-permute-done((bf16[24,2304]{1,0:T(8,128)(2,1)S(1)}, bf16[24,2304]{1,0:T(8,128)(2,1)S(1)}, u32[]{:S(2)}, u32[]{:S(2)}) %collective-permute-start.29) | collective-permute-done | bytes 110624 | tf_op jit(solution)/shard_map/ppermute | solution.py:553
  91.9 1.6 %shard_map.194.refs_7_ = f32[12,48]{1,0:T(8,128)S(1)} custom-call(bf16[24,2304]{1,0:T(8,128)(2,1)S(1)} %collective-permute-done.24.refs_0_, bf16[24,2304]{1,0:T(8,128)(2,1)S(1)} %collective-permute-done.28.refs_1_, bf16[48,2304]{1,0:T(8,128)(2,1)S(1)} %collective-permute-done.33.refs_2_, bf16[24,2304]{1,0:T(8,128)(2,1)S(1)} %collective-permute-done.39.refs_3_, ...), custom_call_target="tpu_custom_call" | custom-call | flops 905969664 | bytes 9059696 | tf_op jit(solution)/shard_map/pallas_call | solution.py:717
  95.1 11.3 %all_to_all.11 = f32[32,4,128]{2,1,0:T(4,128)S(1)} all-to-all(f32[32,4,128]{2,1,0:T(4,128)S(1)} %bitcast.4), channel_id=1, replica_groups=mesh['batch'=8,'vocab'=4] {'batch','vocab'}, dimensions={0} | all-to-all | bytes 131072 | tf_op jit(solution)/shard_map/all_to_all | solution.py:743
  (114 shorter events, 32.4 us)
Async XLA Ops:
  16.4 9.7 %collective-permute-start.11 = (bf16[24,2304]{1,0:T(8,128)(2,1)S(1)}, bf16[24,2304]{1,0:T(8,128)(2,1)S(1)}, u32[]{:S(2)}, u32[]{:S(2)}) collective-permute-start(bf16[24,2304]{1,0:T(8,128)(2,1)S(1)} %get-tuple-element.65), channel_id=1, source_target_pairs={{0,16},{4,20},{8,24},{12,28},{16,0},{20,4},{24,8},{28,12},{1,17},{... | collective-permute-start | bytes 331784 | tf_op jit(solution)/shard_map/ppermute | solution.py:545
  19.1 7.0 %collective-permute-start.12 = (bf16[24,2304]{1,0:T(8,128)(2,1)S(1)}, bf16[24,2304]{1,0:T(8,128)(2,1)S(1)}, u32[]{:S(2)}, u32[]{:S(2)}) collective-permute-start(bf16[24,2304]{1,0:T(8,128)(2,1)S(1)} %get-tuple-element.66), channel_id=1, source_target_pairs={{0,24},{4,28},{8,16},{12,20},{16,8},{20,12},{24,0},{28,4},{1,25},{... | collective-permute-start | bytes 331784 | tf_op jit(solution)/shard_map/ppermute | solution.py:545
  19.1 7.5 %collective-permute-start.13 = (bf16[24,2304]{1,0:T(8,128)(2,1)S(1)}, bf16[24,2304]{1,0:T(8,128)(2,1)S(1)}, u32[]{:S(2)}, u32[]{:S(2)}) collective-permute-start(bf16[24,2304]{1,0:T(8,128)(2,1)S(1)} %get-tuple-element.63.refs_1_), channel_id=1, source_target_pairs={{0,4},{4,0},{8,12},{12,8},{16,20},{20,16},{24,28},{28,24},{1,5},{5... | collective-permute-start | bytes 331784 | tf_op jit(solution)/shard_map/ppermute | solution.py:545
  20.1 6.5 %collective-permute-start.14 = (bf16[24,2304]{1,0:T(8,128)(2,1)S(1)}, bf16[24,2304]{1,0:T(8,128)(2,1)S(1)}, u32[]{:S(2)}, u32[]{:S(2)}) collective-permute-start(bf16[24,2304]{1,0:T(8,128)(2,1)S(1)} %collective-permute-done.10.refs_2_), channel_id=1, source_target_pairs={{0,4},{4,0},{8,12},{12,8},{16,20},{20,16},{24,28},{28,24},{1,5},{5... | collective-permute-start | bytes 331784 | tf_op jit(solution)/shard_map/ppermute | solution.py:545
  29.6 6.0 %collective-permute-start.18 = (bf16[48,2304]{1,0:T(8,128)(2,1)S(1)}, bf16[48,2304]{1,0:T(8,128)(2,1)S(1)}, u32[]{:S(2)}, u32[]{:S(2)}) collective-permute-start(bf16[48,2304]{1,0:T(8,128)(2,1)S(1)} %get-tuple-element.71), channel_id=1, source_target_pairs={{0,1},{1,0},{2,3},{3,2},{4,6},{5,7},{6,4},{7,5},{8,9},{9,8},{10,11... | collective-permute-start | bytes 663560 | tf_op jit(solution)/shard_map/ppermute | solution.py:553
  31.1 7.0 %collective-permute-start.17 = (bf16[48,2304]{1,0:T(8,128)(2,1)S(1)}, bf16[48,2304]{1,0:T(8,128)(2,1)S(1)}, u32[]{:S(2)}, u32[]{:S(2)}) collective-permute-start(bf16[48,2304]{1,0:T(8,128)(2,1)S(1)} %get-tuple-element.70), channel_id=1, source_target_pairs={{0,1},{1,0},{2,3},{3,2},{4,6},{5,7},{6,4},{7,5},{8,9},{9,8},{10,11... | collective-permute-start | bytes 663560 | tf_op jit(solution)/shard_map/ppermute | solution.py:553
  35.6 6.0 %collective-permute-start.20 = (bf16[48,2304]{1,0:T(8,128)(2,1)S(1)}, bf16[48,2304]{1,0:T(8,128)(2,1)S(1)}, u32[]{:S(2)}, u32[]{:S(2)}) collective-permute-start(bf16[48,2304]{1,0:T(8,128)(2,1)S(1)} %add.20.kept_second), channel_id=1, source_target_pairs={{0,2},{1,3},{2,0},{3,1},{4,5},{5,4},{6,7},{7,6},{8,10},{9,11},{10,... | collective-permute-start | bytes 663560 | tf_op jit(solution)/shard_map/ppermute | solution.py:553
  38.2 6.0 %collective-permute-start.19 = (bf16[48,2304]{1,0:T(8,128)(2,1)S(1)}, bf16[48,2304]{1,0:T(8,128)(2,1)S(1)}, u32[]{:S(2)}, u32[]{:S(2)}) collective-permute-start(bf16[48,2304]{1,0:T(8,128)(2,1)S(1)} %add.19.kept_first), channel_id=1, source_target_pairs={{0,2},{1,3},{2,0},{3,1},{4,5},{5,4},{6,7},{7,6},{8,10},{9,11},{10,... | collective-permute-start | bytes 663560 | tf_op jit(solution)/shard_map/ppermute | solution.py:553
  56.0 7.7 %collective-permute-start.32 = (bf16[24,2304]{1,0:T(8,128)(2,1)S(1)}, bf16[24,2304]{1,0:T(8,128)(2,1)S(1)}, u32[]{:S(2)}, u32[]{:S(2)}) collective-permute-start(bf16[24,2304]{1,0:T(8,128)(2,1)S(1)} %shard_map.191.refs_0_), channel_id=1, source_target_pairs={{0,24},{4,28},{8,16},{12,20},{16,8},{20,12},{24,0},{28,4},{1,25},{... | collective-permute-start | bytes 331784 | tf_op jit(solution)/shard_map/ppermute | solution.py:545
  58.6 8.6 %collective-permute-start.31 = (bf16[24,2304]{1,0:T(8,128)(2,1)S(1)}, bf16[24,2304]{1,0:T(8,128)(2,1)S(1)}, u32[]{:S(2)}, u32[]{:S(2)}) collective-permute-start(bf16[24,2304]{1,0:T(8,128)(2,1)S(1)} %shard_map.191.refs_0_), channel_id=1, source_target_pairs={{0,16},{4,20},{8,24},{12,28},{16,0},{20,4},{24,8},{28,12},{1,17},{... | collective-permute-start | bytes 331784 | tf_op jit(solution)/shard_map/ppermute | solution.py:545
  59.4 9.9 %collective-permute-start.39 = (bf16[24,2304]{1,0:T(8,128)(2,1)S(1)}, bf16[24,2304]{1,0:T(8,128)(2,1)S(1)}, u32[]{:S(2)}, u32[]{:S(2)}) collective-permute-start(bf16[24,2304]{1,0:T(8,128)(2,1)S(1)} %shard_map.191.refs_0_), channel_id=1, source_target_pairs={{0,1},{1,0},{2,3},{3,2},{4,6},{5,7},{6,4},{7,5},{8,9},{9,8},{10,11... | collective-permute-start | bytes 331784 | tf_op jit(solution)/shard_map/ppermute | solution.py:553
  59.9 9.4 %collective-permute-start.27 = (bf16[24,2304]{1,0:T(8,128)(2,1)S(1)}, bf16[24,2304]{1,0:T(8,128)(2,1)S(1)}, u32[]{:S(2)}, u32[]{:S(2)}) collective-permute-start(bf16[24,2304]{1,0:T(8,128)(2,1)S(1)} %shard_map.191.refs_0_), channel_id=1, source_target_pairs={{0,8},{4,12},{8,0},{12,4},{16,24},{20,28},{24,16},{28,20},{1,9},{5... | collective-permute-start | bytes 331784 | tf_op jit(solution)/shard_map/ppermute | solution.py:545
  61.0 8.4 %collective-permute-start.36 = (bf16[24,2304]{1,0:T(8,128)(2,1)S(1)}, bf16[24,2304]{1,0:T(8,128)(2,1)S(1)}, u32[]{:S(2)}, u32[]{:S(2)}) collective-permute-start(bf16[24,2304]{1,0:T(8,128)(2,1)S(1)} %shard_map.191.refs_0_), channel_id=1, source_target_pairs={{0,4},{4,0},{8,12},{12,8},{16,20},{20,16},{24,28},{28,24},{1,5},{5... | collective-permute-start | bytes 331784 | tf_op jit(solution)/shard_map/ppermute | solution.py:545
  67.2 11.4 %collective-permute-start.33 = (bf16[48,2304]{1,0:T(8,128)(2,1)S(1)}, bf16[48,2304]{1,0:T(8,128)(2,1)S(1)}, u32[]{:S(2)}, u32[]{:S(2)}) collective-permute-start(bf16[48,2304]{1,0:T(8,128)(2,1)S(1)} %shard_map.192.refs_2_), channel_id=1, source_target_pairs={{0,2},{1,3},{2,0},{3,1},{4,5},{5,4},{6,7},{7,6},{8,10},{9,11},{10,... | collective-permute-start | bytes 663560 | tf_op jit(solution)/shard_map/ppermute | solution.py:553
  67.8 8.2 %collective-permute-start.24 = (bf16[24,2304]{1,0:T(8,128)(2,1)S(1)}, bf16[24,2304]{1,0:T(8,128)(2,1)S(1)}, u32[]{:S(2)}, u32[]{:S(2)}) collective-permute-start(bf16[24,2304]{1,0:T(8,128)(2,1)S(1)} %shard_map.191.refs_0_), channel_id=1, source_target_pairs={{0,2},{1,3},{2,0},{3,1},{4,5},{5,4},{6,7},{7,6},{8,10},{9,11},{10,... | collective-permute-start | bytes 331784 | tf_op jit(solution)/shard_map/ppermute | solution.py:553
  69.3 6.6 %collective-permute-start.45 = (bf16[24,2304]{1,0:T(8,128)(2,1)S(1)}, bf16[24,2304]{1,0:T(8,128)(2,1)S(1)}, u32[]{:S(2)}, u32[]{:S(2)}) collective-permute-start(bf16[24,2304]{1,0:T(8,128)(2,1)S(1)} %collective-permute-done.39.refs_3_), channel_id=1, source_target_pairs={{0,4},{4,0},{8,12},{12,8},{16,20},{20,16},{24,28},{28,24},{1,5},{5... | collective-permute-start | bytes 331784 | tf_op jit(solution)/shard_map/ppermute | solution.py:545
  69.3 7.2 %collective-permute-start.40 = (bf16[24,2304]{1,0:T(8,128)(2,1)S(1)}, bf16[24,2304]{1,0:T(8,128)(2,1)S(1)}, u32[]{:S(2)}, u32[]{:S(2)}) collective-permute-start(bf16[24,2304]{1,0:T(8,128)(2,1)S(1)} %collective-permute-done.27.refs_1_), channel_id=1, source_target_pairs={{0,1},{1,0},{2,3},{3,2},{4,6},{5,7},{6,4},{7,5},{8,9},{9,8},{10,11... | collective-permute-start | bytes 331784 | tf_op jit(solution)/shard_map/ppermute | solution.py:553
  69.4 7.1 %collective-permute-start.37 = (bf16[24,2304]{1,0:T(8,128)(2,1)S(1)}, bf16[24,2304]{1,0:T(8,128)(2,1)S(1)}, u32[]{:S(2)}, u32[]{:S(2)}) collective-permute-start(bf16[24,2304]{1,0:T(8,128)(2,1)S(1)} %collective-permute-done.27.refs_1_), channel_id=1, source_target_pairs={{0,4},{4,0},{8,12},{12,8},{16,20},{20,16},{24,28},{28,24},{1,5},{5... | collective-permute-start | bytes 331784 | tf_op jit(solution)/shard_map/ppermute | solution.py:545
  75.9 7.1 %collective-permute-start.41 = (bf16[48,2304]{1,0:T(8,128)(2,1)S(1)}, bf16[48,2304]{1,0:T(8,128)(2,1)S(1)}, u32[]{:S(2)}, u32[]{:S(2)}) collective-permute-start(bf16[48,2304]{1,0:T(8,128)(2,1)S(1)} %shard_map.192.refs_2_), channel_id=1, source_target_pairs={{0,1},{1,0},{2,3},{3,2},{4,6},{5,7},{6,4},{7,5},{8,9},{9,8},{10,11... | collective-permute-start | bytes 663560 | tf_op jit(solution)/shard_map/ppermute | solution.py:553
  76.5 6.6 %collective-permute-start.25 = (bf16[24,2304]{1,0:T(8,128)(2,1)S(1)}, bf16[24,2304]{1,0:T(8,128)(2,1)S(1)}, u32[]{:S(2)}, u32[]{:S(2)}) collective-permute-start(bf16[24,2304]{1,0:T(8,128)(2,1)S(1)} %collective-permute-done.24.refs_0_), channel_id=1, source_target_pairs={{0,1},{1,0},{2,3},{3,2},{4,6},{5,7},{6,4},{7,5},{8,9},{9,8},{10,11... | collective-permute-start | bytes 331784 | tf_op jit(solution)/shard_map/ppermute | solution.py:553
  78.6 6.9 %collective-permute-start.34 = (bf16[48,2304]{1,0:T(8,128)(2,1)S(1)}, bf16[48,2304]{1,0:T(8,128)(2,1)S(1)}, u32[]{:S(2)}, u32[]{:S(2)}) collective-permute-start(bf16[48,2304]{1,0:T(8,128)(2,1)S(1)} %collective-permute-done.33.refs_2_), channel_id=1, source_target_pairs={{0,1},{1,0},{2,3},{3,2},{4,6},{5,7},{6,4},{7,5},{8,9},{9,8},{10,11... | collective-permute-start | bytes 663560 | tf_op jit(solution)/shard_map/ppermute | solution.py:553
  83.1 8.8 %collective-permute-start.47 = (bf16[48,2304]{1,0:T(8,128)(2,1)S(1)}, bf16[48,2304]{1,0:T(8,128)(2,1)S(1)}, u32[]{:S(2)}, u32[]{:S(2)}) collective-permute-start(bf16[48,2304]{1,0:T(8,128)(2,1)S(1)} %collective-permute-done.41.refs_5_), channel_id=1, source_target_pairs={{0,4},{4,0},{8,12},{12,8},{16,20},{20,16},{24,28},{28,24},{1,5},{5... | collective-permute-start | bytes 663560 | tf_op jit(solution)/shard_map/ppermute | solution.py:545
  83.6 8.3 %collective-permute-start.44 = (bf16[48,2304]{1,0:T(8,128)(2,1)S(1)}, bf16[48,2304]{1,0:T(8,128)(2,1)S(1)}, u32[]{:S(2)}, u32[]{:S(2)}) collective-permute-start(bf16[48,2304]{1,0:T(8,128)(2,1)S(1)} %collective-permute-done.33.refs_2_), channel_id=1, source_target_pairs={{0,4},{4,0},{8,12},{12,8},{16,20},{20,16},{24,28},{28,24},{1,5},{5... | collective-permute-start | bytes 663560 | tf_op jit(solution)/shard_map/ppermute | solution.py:545
  85.4 8.1 %collective-permute-start.35 = (bf16[48,2304]{1,0:T(8,128)(2,1)S(1)}, bf16[48,2304]{1,0:T(8,128)(2,1)S(1)}, u32[]{:S(2)}, u32[]{:S(2)}) collective-permute-start(bf16[48,2304]{1,0:T(8,128)(2,1)S(1)} %collective-permute-done.34.refs_2_), channel_id=1, source_target_pairs={{0,4},{4,0},{8,12},{12,8},{16,20},{20,16},{24,28},{28,24},{1,5},{5... | collective-permute-start | bytes 663560 | tf_op jit(solution)/shard_map/ppermute | solution.py:545
  (33 other events, 247.4 us)
